TPU v7x, 32 devices: a whole 2x2x4 slice. The times are simulated.
32 devices in a mesh: seq: 8 (over z, x), head: 4 (over y, core).
Axes of the slice: x: 2, y: 2, z: 4, core: 2. Of those that a mesh axis runs over, the one named last changes fastest.
Arguments:
- tokens: bfloat16 [2048, 3584], P('seq'), may hold values from -16 to 16
- length: int32 [1], replicated, may hold values from 512 to 2048
- in_gain: float32 [3584], replicated, may hold values from 0.5 to 1.5
- q_weight: bfloat16 [3584, 3584], P(None, 'head'), may hold values from -0.09375 to 0.09375
- q_bias: float32 [3584], P('head'), may hold values from -60 to 60
- k_weight: bfloat16 [3584, 512], P(None, 'head'), may hold values from -0.09375 to 0.09375
- k_bias: float32 [512], P('head'), may hold values from -60 to 60
- v_weight: bfloat16 [3584, 512], P(None, 'head'), may hold values from -0.09375 to 0.09375
- v_bias: float32 [512], P('head'), may hold values from -2 to 2
- o_weight: bfloat16 [3584, 3584], P('head'), may hold values from -0.125 to 0.125
- final_gain: float32 [3584], P('head'), may hold values from 0.5 to 1.5
Outputs:
- hidden: bfloat16 [2048, 3584], P('seq', 'head')
- embedding: float32 [3584], P('head')
All inputs are finite; a program needn't handle non-finite values.
Results may differ from a plain program's by a relative error of at most 0.0075.
The roundings to bfloat16 on the way count: a program that leaves them out, or rounds other values in their place, can miss the bound.
Values may be sent and summed in bfloat16 or wider, within the bound.
A program may use at most 192 MiB of HBM per device.

v0:
```python
import functools

import jax
import jax.numpy as jnp
import numpy as np
from jax import lax
from jax.experimental import pallas as pl
from jax.experimental.pallas import tpu as pltpu
from jax.sharding import PartitionSpec as P

HEAD_DIM = 128
ROPE_BASE = 1000000.0
EPS = 1e-06
MESH = pl.DeviceIdType.MESH
F32 = jnp.float32
BF16 = jnp.bfloat16
LOW = -1e30


def widths(share):
    out, at = [], 0
    first = share % 256 or 256
    while at < share:
        width = first if at == 0 else 256
        out.append((1, at, width))
        at += width
    cut = out[len(out) // 2][1]
    return [(0, 0, cut), (0, cut, share - cut)] + out


def dot(a, b):
    return jnp.dot(a, b, preferred_element_type=F32)


def kernel(
    n_seq,
    n_head,
    length_ref,
    tokens_hbm,
    gain_1d,
    wq_hbm,
    qb_1d,
    wk_hbm,
    kb_1d,
    wv_hbm,
    vb_1d,
    wo_hbm,
    fgain_1d,
    cos_row,
    sin_row,
    cos_off,
    sin_off,
    hidden_hbm,
    emb_ref,
    gain_ref,
    qb_ref,
    kb_ref,
    vb_ref,
    fgain_ref,
    tok,
    normed,
    wkv,
    wq,
    wo,
    cos,
    sin,
    qt,
    kbuf,
    vbuf,
    m_ref,
    l_ref,
    acc_ref,
    att,
    hid,
    hid_bf,
    sqbuf,
    pbuf,
    wbuf,
    local_sem,
    ring_send,
    ring_recv,
    pair_send,
    pair_recv,
    cross_send,
    cross_recv,
    sq_send,
    sq_recv,
    pool_send,
    pool_recv,
    pow_send,
    pow_recv,
    *chunk_bufs,
):
    rows, width = tok.shape
    share = hid.shape[1]
    heads = qt.shape[2] // (rows // 2)
    part_rows = rows // 2
    half = n_seq // 2
    n_y = n_head // 2
    chunks = widths(share)
    psend, precv = chunk_bufs[0::5], chunk_bufs[1::5]
    pown, ysend, yrecv = chunk_bufs[2::5], chunk_bufs[3::5], chunk_bufs[4::5]
    ms = lax.axis_index("seq")
    mh = lax.axis_index("head")
    limit = length_ref[0]

    loads = [
        pltpu.make_async_copy(tokens_hbm, tok, local_sem.at[0]),
        pltpu.make_async_copy(wk_hbm, wkv.at[:, :HEAD_DIM], local_sem.at[1]),
        pltpu.make_async_copy(wv_hbm, wkv.at[:, HEAD_DIM:], local_sem.at[2]),
        pltpu.make_async_copy(wq_hbm, wq, local_sem.at[3]),
        pltpu.make_async_copy(wo_hbm, wo, local_sem.at[4]),
    ]
    for load in loads[:4]:
        load.start()

    for flat, row in (
        (gain_1d, gain_ref),
        (qb_1d, qb_ref),
        (kb_1d, kb_ref),
        (vb_1d, vb_ref),
        (fgain_1d, fgain_ref),
    ):
        for g in range(0, row.shape[1], HEAD_DIM):
            row[:, g : g + HEAD_DIM] = flat[g : g + HEAD_DIM].reshape(1, HEAD_DIM)

    barrier = pltpu.get_barrier_semaphore()

    def greet(d, carry):
        pl.semaphore_signal(
            barrier, inc=1, device_id={"seq": lax.rem(ms + d, n_seq)}, device_id_type=MESH
        )
        return carry

    lax.fori_loop(1, n_seq, greet, 0)
    for d in range(1, n_head):
        pl.semaphore_signal(
            barrier, inc=1, device_id={"head": lax.rem(mh + d, n_head)}, device_id_type=MESH
        )

    far = pl.ds(pl.multiple_of(ms * 8, 8), 8)
    co, so = cos_off[far, :][:1], sin_off[far, :][:1]
    lane = lax.broadcasted_iota(jnp.int32, (1, HEAD_DIM), 1)
    sign = jnp.where(lane < HEAD_DIM // 2, -1.0, 1.0)
    cos[...] = cos_row[...] * co - sin_row[...] * so
    sin[...] = (sin_row[...] * co + cos_row[...] * so) * sign

    def rope(u):
        return u * cos[...] + pltpu.roll(u, HEAD_DIM // 2, 1) * sin[...]

    loads[0].wait()
    block = 16

    def norm_block(i, carry):
        at = pl.ds(pl.multiple_of(i * block, block), block)
        x = tok[at, :].astype(F32)
        mean = jnp.sum(x * x, axis=1, keepdims=True) / width
        normed[at, :] = (x * lax.rsqrt(mean + EPS) * gain_ref[...]).astype(BF16)
        return carry

    lax.fori_loop(0, rows // block, norm_block, 0)

    loads[1].wait()
    loads[2].wait()
    kv = dot(normed[...], wkv[...])
    kbuf[ms] = rope(kv[:, :HEAD_DIM] + kb_ref[...]).astype(BF16)
    vbuf[ms] = jnp.transpose(kv[:, HEAD_DIM:] + vb_ref[...]).astype(BF16)

    q2 = lax.div(ms, 2)
    pos = q2 + (ms - 2 * q2) * (n_seq - 1 - 2 * q2)

    def slot(p):
        p = lax.rem(p + 2 * n_seq, n_seq)
        back = lax.div(p, half)
        return (1 - back) * 2 * p + back * (2 * (n_seq - 1 - p) + 1)

    ends = (slot(pos + 1), slot(pos - 1))

    def moved(way, kind, s, hops):
        sign_of = 1 if way == 0 else -1
        at = slot(pos - sign_of * hops)
        buf = vbuf if kind else kbuf
        return pltpu.make_async_remote_copy(
            src_ref=buf.at[at],
            dst_ref=buf.at[at],
            send_sem=ring_send.at[2 * way + kind, s],
            recv_sem=ring_recv.at[2 * way + kind, s],
            device_id={"seq": ends[way]},
            device_id_type=MESH,
        )

    def send(way, kind, s):
        return moved(way, kind, s, s - 1)

    def arrival(way, kind, s):
        return moved(way, kind, s, s)

    pl.semaphore_wait(barrier, n_seq + n_head - 2)
    for kind in (0, 1):
        for way in (0, 1):
            send(way, kind, 1).start()

    def put_query(h, u):
        at = pl.ds(pl.multiple_of(h * HEAD_DIM, HEAD_DIM), HEAD_DIM)
        to = pl.ds(pl.multiple_of(h * part_rows, part_rows), part_rows)
        u = rope(u + qb_ref[:, at]) * HEAD_DIM ** (-0.5)
        u = jnp.transpose(u).astype(BF16)
        qt[0, :, to] = u[:, :part_rows]
        qt[1, :, to] = u[:, part_rows:]

    loads[3].wait()
    loads[4].start()

    def query_pair(j, carry):
        at = pl.ds(pl.multiple_of(j * 2 * HEAD_DIM, 2 * HEAD_DIM), 2 * HEAD_DIM)
        u = dot(normed[...], wq[:, at])
        put_query(2 * j, u[:, :HEAD_DIM])
        put_query(2 * j + 1, u[:, HEAD_DIM:])
        return carry

    lax.fori_loop(0, heads // 2, query_pair, 0)
    if heads % 2:
        put_query(heads - 1, dot(normed[...], wq[:, (heads - 1) * HEAD_DIM :]))

    m_ref[...] = jnp.full(m_ref.shape, LOW, F32)
    l_ref[...] = jnp.zeros(l_ref.shape, F32)
    acc_ref[...] = jnp.zeros(acc_ref.shape, F32)
    lanes = heads * part_rows
    tiles = [(t, min(256, lanes - t)) for t in range(0, lanes, 256)]

    def attend(part, blocks):
        row_at = lax.broadcasted_iota(jnp.int32, (rows, 1), 0)
        live = [b * rows + row_at < limit for b in blocks]
        for t, wide in tiles:
            at = slice(t, t + wide)
            query = qt[part, :, at]
            scores = [jnp.where(ok, dot(kbuf[b], query), LOW) for b, ok in zip(blocks, live)]
            tops = [jnp.max(s, axis=0, keepdims=True) for s in scores]
            old = m_ref[part, :, at][:1]
            top = functools.reduce(jnp.maximum, tops, old)
            alpha = jnp.exp(old - top)
            total = l_ref[part, :, at][:1] * alpha
            mixed = acc_ref[part, :, at] * alpha
            for b, s in zip(blocks, scores):
                p = jnp.exp(s - top)
                total = total + jnp.sum(p, axis=0, keepdims=True)
                mixed = mixed + dot(vbuf[b], p.astype(BF16))
            m_ref[part, :, at] = jnp.broadcast_to(top, (8, wide))
            l_ref[part, :, at] = jnp.broadcast_to(total, (8, wide))
            acc_ref[part, :, at] = mixed

    def forward(s, kinds_ways):
        for kind in (0, 1):
            for way in (0, 1):
                arrival(way, kind, s).wait_recv()
                if (way, kind) in kinds_ways:
                    send(way, kind, s + 1).start()

    every = ((0, 0), (0, 1), (1, 0), (1, 1))
    last = ((0, 0), (1, 1))
    forward(1, every if half > 2 else last)
    attend(0, [ms])
    attend(0, [slot(pos - 1), slot(pos + 1)])

    def ring_step(s, carry):
        forward(s, every)
        attend(0, [slot(pos - s), slot(pos + s)])
        return carry

    if half > 3:
        lax.fori_loop(2, half - 1, ring_step, 0)
    if half > 2:
        forward(half - 1, last)
        attend(0, [slot(pos - half + 1), slot(pos + half - 1)])
    for way, kind in last:
        arrival(way, kind, half).wait_recv()
    attend(0, [slot(pos - half)])

    def finish(part):
        for h in range(heads):
            at = slice(h * part_rows, (h + 1) * part_rows)
            done = jnp.transpose(acc_ref[part, :, at] / l_ref[part, :, at][:1]).astype(BF16)
            cols = slice(h * HEAD_DIM, (h + 1) * HEAD_DIM)
            att[part * part_rows : (part + 1) * part_rows, cols] = done

    loads[4].wait()
    my = lax.div(mh, 2)
    mc = mh - 2 * my
    partner = 2 * my + 1 - mc

    def partial(part, dest, at, wide):
        cols = pl.ds(pl.multiple_of(dest * share + at, HEAD_DIM), wide)
        return dot(att[part * part_rows : (part + 1) * part_rows, :], wo[:, cols])

    def pair_copy(i):
        return pltpu.make_async_remote_copy(
            src_ref=psend[i],
            dst_ref=precv[i],
            send_sem=pair_send.at[i],
            recv_sem=pair_recv.at[i],
            device_id={"head": partner},
            device_id_type=MESH,
        )

    def cross_copy(i, d):
        return pltpu.make_async_remote_copy(
            src_ref=ysend[i].at[d - 1],
            dst_ref=yrecv[i].at[d - 1],
            send_sem=cross_send.at[i, d - 1],
            recv_sem=cross_recv.at[i, d - 1],
            device_id={"head": 2 * lax.rem(my + d, n_y) + mc},
            device_id_type=MESH,
        )

    def to_partner(i):
        part, at, wide = chunks[i]
        for y in range(n_y):
            psend[i][y] = partial(part, 2 * y + 1 - mc, at, wide).astype(BF16)
        pair_copy(i).start()
        for d in range(1, n_y):
            pown[i][d] = partial(part, 2 * lax.rem(my + d, n_y) + mc, at, wide)

    def across(i):
        pair_copy(i).wait_recv()
        for d in range(1, n_y):
            y = lax.rem(my + d, n_y)
            ysend[i][d - 1] = (pown[i][d] + precv[i][y].astype(F32)).astype(BF16)
            cross_copy(i, d).start()

    early = [i for i, c in enumerate(chunks) if c[0] == 0]
    late = [i for i, c in enumerate(chunks) if c[0] == 1]
    finish(0)
    for i in early:
        to_partner(i)
    attend(1, [0, 1])
    for i in early:
        across(i)

    def whole_step(i, carry):
        attend(1, [2 * i, 2 * i + 1])
        return carry

    lax.fori_loop(1, half, whole_step, 0)
    finish(1)
    for i in late:
        to_partner(i)
        if i > late[0]:
            across(i - 1)
    across(late[-1])
    for i, (part, at, wide) in enumerate(chunks):
        pown[i][0] = partial(part, mh, at, wide)

    squares = [None, None]
    for i, (part, at, wide) in enumerate(chunks):
        mine = pl.ds(pl.multiple_of(mh * share + at, HEAD_DIM), wide)
        band = slice(part * part_rows, (part + 1) * part_rows)
        base = tok[band, mine].astype(F32) + (pown[i][0] + precv[i][my].astype(F32))
        for d in range(1, n_y):
            cross_copy(i, d).wait_recv()
            base = base + yrecv[i][d - 1].astype(F32)
        hid[band, at : at + wide] = base
        hid_bf[band, at : at + wide] = base.astype(BF16)
        for g in range(0, wide, HEAD_DIM):
            piece = base[:, g : g + HEAD_DIM]
            more = piece * piece
            squares[part] = more if squares[part] is None else squares[part] + more
    squares = jnp.concatenate(squares, axis=0)
    out_copy = pltpu.make_async_copy(hid_bf, hidden_hbm, local_sem.at[5])
    out_copy.start()

    def head_copy(buf, send_sems, recv_sems, d):
        return pltpu.make_async_remote_copy(
            src_ref=buf.at[mh],
            dst_ref=buf.at[mh],
            send_sem=send_sems.at[d - 1],
            recv_sem=recv_sems.at[d - 1],
            device_id={"head": lax.rem(mh + d, n_head)},
            device_id_type=MESH,
        )

    def head_arrival(buf, send_sems, recv_sems, d):
        source = lax.rem(mh + n_head - d, n_head)
        return pltpu.make_async_remote_copy(
            src_ref=buf.at[source],
            dst_ref=buf.at[source],
            send_sem=send_sems.at[d - 1],
            recv_sem=recv_sems.at[d - 1],
            device_id={"head": source},
            device_id_type=MESH,
        )

    def head_sum(buf, send_sems, recv_sems, value):
        buf[mh] = jnp.broadcast_to(value, buf.shape[1:])
        for d in range(1, n_head):
            head_copy(buf, send_sems, recv_sems, d).start()
        for d in range(1, n_head):
            head_arrival(buf, send_sems, recv_sems, d).wait_recv()
        return functools.reduce(lambda a, b: a + b, [buf[d][:1] for d in range(n_head)])

    square_row = jnp.sum(jnp.transpose(squares), axis=0, keepdims=True)
    power = head_sum(sqbuf, sq_send, sq_recv, square_row)
    place = ms * rows + lax.broadcasted_iota(jnp.int32, (1, rows), 1)
    scale = jnp.where(place < limit, lax.rsqrt(power / width + EPS), 0.0)
    scale = jnp.transpose(jnp.broadcast_to(scale, (HEAD_DIM, rows)))

    groups = pbuf.shape[1]
    sums = []
    for g in range(0, share, HEAD_DIM):
        at = slice(g, g + HEAD_DIM)
        sums.append(jnp.sum(hid[:, at] * scale, axis=0, keepdims=True) * fgain_ref[:, at])
    sums += [jnp.zeros((1, HEAD_DIM), F32)] * (groups - len(sums))
    pbuf[ms] = jnp.concatenate(sums, axis=0)

    def pool_copy(d):
        return pltpu.make_async_remote_copy(
            src_ref=pbuf.at[ms],
            dst_ref=pbuf.at[ms],
            send_sem=pool_send.at[d - 1],
            recv_sem=pool_recv.at[d - 1],
            device_id={"seq": lax.rem(ms + d, n_seq)},
            device_id_type=MESH,
        )

    def pool_start(d, carry):
        pool_copy(d).start()
        return carry

    def pool_wait(d, carry):
        source = lax.rem(ms + n_seq - d, n_seq)
        pltpu.make_async_remote_copy(
            src_ref=pbuf.at[source],
            dst_ref=pbuf.at[source],
            send_sem=pool_send.at[d - 1],
            recv_sem=pool_recv.at[d - 1],
            device_id={"seq": source},
            device_id_type=MESH,
        ).wait_recv()
        return carry

    lax.fori_loop(1, n_seq, pool_start, 0)
    lax.fori_loop(1, n_seq, pool_wait, 0)
    mean = functools.reduce(lambda a, b: a + b, [pbuf[d] for d in range(n_seq)])
    mean = mean / limit.astype(F32)
    total = head_sum(wbuf, pow_send, pow_recv, jnp.sum(mean * mean, axis=0, keepdims=True))
    pooled = mean * lax.rsqrt(jnp.sum(total, axis=1, keepdims=True) / width + EPS)
    for g in range(share // HEAD_DIM):
        emb_ref[g * HEAD_DIM : (g + 1) * HEAD_DIM] = pooled[g : g + 1].reshape(HEAD_DIM)

    def sent(s, carry):
        for way, kind in every:
            send(way, kind, s).wait_send()
        return carry

    lax.fori_loop(1, half, sent, 0)
    for way, kind in last:
        send(way, kind, half).wait_send()
    for i in range(len(chunks)):
        pair_copy(i).wait_send()
        for d in range(1, n_y):
            cross_copy(i, d).wait_send()
    for d in range(1, n_head):
        head_copy(sqbuf, sq_send, sq_recv, d).wait_send()
        head_copy(wbuf, pow_send, pow_recv, d).wait_send()

    def pool_sent(d, carry):
        pool_copy(d).wait_send()
        return carry

    lax.fori_loop(1, n_seq, pool_sent, 0)
    out_copy.wait()


def body(
    n_seq,
    n_head,
    tokens,
    length,
    in_gain,
    q_weight,
    q_bias,
    k_weight,
    k_bias,
    v_weight,
    v_bias,
    o_weight,
    final_gain,
):
    rows, width = tokens.shape
    share = width // n_head
    heads = q_weight.shape[1] // HEAD_DIM
    half = n_seq // 2
    n_y = n_head // 2
    inverse = ROPE_BASE ** (-(np.arange(HEAD_DIM // 2) * 2.0) / HEAD_DIM)
    inverse = np.concatenate([inverse, inverse])[None, :]
    near = np.arange(rows)[:, None] * inverse
    far = np.repeat(np.arange(n_seq) * rows, 8)[:, None] * inverse
    tables = [f(a).astype(np.float32) for a in (near, far) for f in (np.cos, np.sin)]

    chunks = widths(share)
    groups = -(-share // (8 * HEAD_DIM)) * 8
    chunk_bufs = []
    for _, _, wide in chunks:
        chunk_bufs += [
            pltpu.VMEM((n_y, rows // 2, wide), BF16),
            pltpu.VMEM((n_y, rows // 2, wide), BF16),
            pltpu.VMEM((n_y, rows // 2, wide), F32),
            pltpu.VMEM((n_y - 1, rows // 2, wide), BF16),
            pltpu.VMEM((n_y - 1, rows // 2, wide), BF16),
        ]
    dma = pltpu.SemaphoreType.DMA
    hbm = pl.BlockSpec(memory_space=pl.ANY)
    vmem = pl.BlockSpec(memory_space=pltpu.VMEM)
    smem = pl.BlockSpec(memory_space=pltpu.SMEM)
    hidden, embedding = pl.pallas_call(
        functools.partial(kernel, n_seq, n_head),
        out_shape=(
            jax.ShapeDtypeStruct((rows, share), BF16),
            jax.ShapeDtypeStruct((share,), F32),
        ),
        in_specs=[smem, hbm, vmem, hbm, vmem, hbm, vmem, hbm, vmem, hbm] + [vmem] * 5,
        out_specs=(hbm, vmem),
        scratch_shapes=[
            pltpu.VMEM((1, width), F32),
            pltpu.VMEM((1, heads * HEAD_DIM), F32),
            pltpu.VMEM((1, HEAD_DIM), F32),
            pltpu.VMEM((1, HEAD_DIM), F32),
            pltpu.VMEM((1, share), F32),
            pltpu.VMEM((rows, width), BF16),
            pltpu.VMEM((rows, width), BF16),
            pltpu.VMEM((width, 2 * HEAD_DIM), BF16),
            pltpu.VMEM(q_weight.shape, BF16),
            pltpu.VMEM(o_weight.shape, BF16),
            pltpu.VMEM((rows, HEAD_DIM), F32),
            pltpu.VMEM((rows, HEAD_DIM), F32),
            pltpu.VMEM((2, HEAD_DIM, heads * (rows // 2)), BF16),
            pltpu.VMEM((n_seq, rows, HEAD_DIM), BF16),
            pltpu.VMEM((n_seq, HEAD_DIM, rows), BF16),
            pltpu.VMEM((2, 8, heads * (rows // 2)), F32),
            pltpu.VMEM((2, 8, heads * (rows // 2)), F32),
            pltpu.VMEM((2, HEAD_DIM, heads * (rows // 2)), F32),
            pltpu.VMEM((rows, heads * HEAD_DIM), BF16),
            pltpu.VMEM((rows, share), F32),
            pltpu.VMEM((rows, share), BF16),
            pltpu.VMEM((n_head, 8, rows), F32),
            pltpu.VMEM((n_seq, groups, HEAD_DIM), F32),
            pltpu.VMEM((n_head, 8, HEAD_DIM), F32),
            dma((6,)),
            dma((4, half + 1)),
            dma((4, half + 1)),
            dma((len(chunks),)),
            dma((len(chunks),)),
            dma((len(chunks), n_y)),
            dma((len(chunks), n_y)),
            dma((n_head,)),
            dma((n_head,)),
            dma((n_seq,)),
            dma((n_seq,)),
            dma((n_head,)),
            dma((n_head,)),
        ]
        + chunk_bufs,
        compiler_params=pltpu.CompilerParams(
            collective_id=0, has_side_effects=True, vmem_limit_bytes=60 * 1024 * 1024
        ),
    )(
        length,
        tokens,
        in_gain,
        q_weight,
        q_bias,
        k_weight,
        k_bias,
        v_weight,
        v_bias,
        o_weight,
        final_gain,
        *tables,
    )
    return hidden, embedding


def solution(mesh):
    in_specs = (
        P("seq", None),
        P(),
        P(),
        P(None, "head"),
        P("head"),
        P(None, "head"),
        P("head"),
        P(None, "head"),
        P("head"),
        P("head", None),
        P("head"),
    )
    out_specs = (P("seq", "head"), P("head"))
    step = functools.partial(body, mesh.shape["seq"], mesh.shape["head"])
    return jax.shard_map(step, mesh=mesh, in_specs=in_specs, out_specs=out_specs, check_vma=False)
```

profile of v0, /device:TPU:0, one launch (start us, length us, event | category | flops | bytes accessed | tf_op | source)
XLA Modules:
  0.0 56.6 jit_solution(8124690687570446369)
XLA Ops:
  1.3 52.3 %shard_map.158 = (bf16[256,896]{1,0:T(8,128)(2,1)}, f32[896]{0:T(1024)}) custom-call(s32[1]{0:T(128)S(6)} %copy.19.length_ref, bf16[256,3584]{1,0:T(8,128)(2,1)} %tokens_hbm.1, f32[3584]{0:T(1024)} %gain_1d.1, bf16[3584,896]{1,0:T(8,128)(2,1)} %wq_hbm.1, f32[896]{0:T(1024)} %qb_1d.1, bf16[3584,128]{1,0:T(8,128)(2,1)} %wk_hbm.1, f32[128]{0:T(128)} %kb_1d.1, ...), custom_call_target="tpu_custom_call" | custom-call | tf_op jit(solution)/shard_map/pallas_call | solution.py:514
  53.5 1.8 %copy.20 = bf16[256,896]{1,0:T(8,128)(2,1)} copy(bf16[256,896]{1,0:T(8,128)(2,1)} %get-tuple-element.4) | data formatting | bytes 917504
  55.4 1.3 %copy.21 = f32[896]{0:T(1024)} copy(f32[896]{0:T(1024)} %get-tuple-element.5) | data formatting | bytes 7168
where the time goes:
time: 56.9 us; the launch traced here: 56.6 us
  Pallas kernels  52.3 us (92%)
  local copies, waits for them, and re-layouts  3.09 us (5%)
  between operations  1.29 us (2%)
    pallas_call x1, Pallas kernels, body(): pl.pallas_call(functools.partial(kernel, n_seq, n_head), out_shape=(jax.S...  52.3 us
    unnamed x2, local copies, waits for them, and re-layouts  3.09 us

commit v1 on v0

--- a/solution.py
+++ b/solution.py
@@ -35,23 +35,29 @@
 def kernel(
     n_seq,
     n_head,
+    length_hbm,
+    tokens_hbm,
+    gain_hbm,
+    wq_hbm,
+    qb_hbm,
+    wk_hbm,
+    kb_hbm,
+    wv_hbm,
+    vb_hbm,
+    wo_hbm,
+    fgain_hbm,
+    near_hbm,
+    far_hbm,
+    hid_bf,
+    emb_ref,
     length_ref,
-    tokens_hbm,
     gain_1d,
-    wq_hbm,
     qb_1d,
-    wk_hbm,
     kb_1d,
-    wv_hbm,
     vb_1d,
-    wo_hbm,
     fgain_1d,
-    cos_row,
-    sin_row,
-    cos_off,
-    sin_off,
-    hidden_hbm,
-    emb_ref,
+    near,
+    far,
     gain_ref,
     qb_ref,
     kb_ref,
@@ -72,7 +78,6 @@
     acc_ref,
     att,
     hid,
-    hid_bf,
     sqbuf,
     pbuf,
     wbuf,
@@ -102,7 +107,6 @@
     pown, ysend, yrecv = chunk_bufs[2::5], chunk_bufs[3::5], chunk_bufs[4::5]
     ms = lax.axis_index("seq")
     mh = lax.axis_index("head")
-    limit = length_ref[0]
 
     loads = [
         pltpu.make_async_copy(tokens_hbm, tok, local_sem.at[0]),
@@ -111,9 +115,42 @@
         pltpu.make_async_copy(wq_hbm, wq, local_sem.at[3]),
         pltpu.make_async_copy(wo_hbm, wo, local_sem.at[4]),
     ]
-    for load in loads[:4]:
+    smalls = [
+        pltpu.make_async_copy(near_hbm, near, local_sem.at[5]),
+        pltpu.make_async_copy(far_hbm.at[ms], far, local_sem.at[6]),
+        pltpu.make_async_copy(gain_hbm, gain_1d, local_sem.at[7]),
+        pltpu.make_async_copy(kb_hbm, kb_1d, local_sem.at[8]),
+        pltpu.make_async_copy(vb_hbm, vb_1d, local_sem.at[9]),
+        pltpu.make_async_copy(qb_hbm, qb_1d, local_sem.at[10]),
+        pltpu.make_async_copy(fgain_hbm, fgain_1d, local_sem.at[11]),
+        pltpu.make_async_copy(length_hbm, length_ref, local_sem.at[12]),
+    ]
+    loads[0].start()
+    for small in smalls:
+        small.start()
+    for load in loads[1:4]:
         load.start()
 
+    barrier = pltpu.get_barrier_semaphore()
+
+    def greet(d, carry):
+        pl.semaphore_signal(
+            barrier, inc=1, device_id={"seq": lax.rem(ms + d, n_seq)}, device_id_type=MESH
+        )
+        return carry
+
+    lax.fori_loop(1, n_seq, greet, 0)
+    for d in range(1, n_head):
+        pl.semaphore_signal(
+            barrier, inc=1, device_id={"head": lax.rem(mh + d, n_head)}, device_id_type=MESH
+        )
+
+    def rope(u):
+        return u * cos[...] + pltpu.roll(u, HEAD_DIM // 2, 1) * sin[...]
+
+    for small in smalls:
+        small.wait()
+    limit = length_ref[0]
     for flat, row in (
         (gain_1d, gain_ref),
         (qb_1d, qb_ref),
@@ -124,29 +161,11 @@
         for g in range(0, row.shape[1], HEAD_DIM):
             row[:, g : g + HEAD_DIM] = flat[g : g + HEAD_DIM].reshape(1, HEAD_DIM)
 
-    barrier = pltpu.get_barrier_semaphore()
-
-    def greet(d, carry):
-        pl.semaphore_signal(
-            barrier, inc=1, device_id={"seq": lax.rem(ms + d, n_seq)}, device_id_type=MESH
-        )
-        return carry
-
-    lax.fori_loop(1, n_seq, greet, 0)
-    for d in range(1, n_head):
-        pl.semaphore_signal(
-            barrier, inc=1, device_id={"head": lax.rem(mh + d, n_head)}, device_id_type=MESH
-        )
-
-    far = pl.ds(pl.multiple_of(ms * 8, 8), 8)
-    co, so = cos_off[far, :][:1], sin_off[far, :][:1]
     lane = lax.broadcasted_iota(jnp.int32, (1, HEAD_DIM), 1)
     sign = jnp.where(lane < HEAD_DIM // 2, -1.0, 1.0)
-    cos[...] = cos_row[...] * co - sin_row[...] * so
-    sin[...] = (sin_row[...] * co + cos_row[...] * so) * sign
-
-    def rope(u):
-        return u * cos[...] + pltpu.roll(u, HEAD_DIM // 2, 1) * sin[...]
+    co, so = far[0, :1], far[1, :1]
+    cos[...] = near[0] * co - near[1] * so
+    sin[...] = (near[1] * co + near[0] * so) * sign
 
     loads[0].wait()
     block = 16
@@ -365,8 +384,6 @@
             more = piece * piece
             squares[part] = more if squares[part] is None else squares[part] + more
     squares = jnp.concatenate(squares, axis=0)
-    out_copy = pltpu.make_async_copy(hid_bf, hidden_hbm, local_sem.at[5])
-    out_copy.start()
 
     def head_copy(buf, send_sems, recv_sems, d):
         return pltpu.make_async_remote_copy(
@@ -467,7 +484,17 @@
         return carry
 
     lax.fori_loop(1, n_seq, pool_sent, 0)
-    out_copy.wait()
+
+
+def write_out(hidden_ref, emb_ref, hidden_hbm, emb_hbm, sems):
+    copies = [
+        pltpu.make_async_copy(hidden_ref, hidden_hbm, sems.at[0]),
+        pltpu.make_async_copy(emb_ref, emb_hbm, sems.at[1]),
+    ]
+    for copy in copies:
+        copy.start()
+    for copy in copies:
+        copy.wait()
 
 
 def body(
@@ -493,8 +520,10 @@
     inverse = ROPE_BASE ** (-(np.arange(HEAD_DIM // 2) * 2.0) / HEAD_DIM)
     inverse = np.concatenate([inverse, inverse])[None, :]
     near = np.arange(rows)[:, None] * inverse
-    far = np.repeat(np.arange(n_seq) * rows, 8)[:, None] * inverse
-    tables = [f(a).astype(np.float32) for a in (near, far) for f in (np.cos, np.sin)]
+    near = np.stack([np.cos(near), np.sin(near)]).astype(np.float32)
+    far = (np.arange(n_seq) * rows)[:, None] * inverse
+    far = np.stack([np.cos(far), np.sin(far)], axis=1).astype(np.float32)
+    far = np.repeat(far[:, :, None, :], 8, axis=2)
 
     chunks = widths(share)
     groups = -(-share // (8 * HEAD_DIM)) * 8
@@ -508,18 +537,41 @@
             pltpu.VMEM((n_y - 1, rows // 2, wide), BF16),
         ]
     dma = pltpu.SemaphoreType.DMA
-    hbm = pl.BlockSpec(memory_space=pl.ANY)
+    hbm = pl.BlockSpec(memory_space=pltpu.HBM)
     vmem = pl.BlockSpec(memory_space=pltpu.VMEM)
-    smem = pl.BlockSpec(memory_space=pltpu.SMEM)
+    shapes = (
+        jax.ShapeDtypeStruct((rows, share), BF16),
+        jax.ShapeDtypeStruct((share,), F32),
+    )
+    operands = (
+        length,
+        tokens,
+        in_gain,
+        q_weight,
+        q_bias,
+        k_weight,
+        k_bias,
+        v_weight,
+        v_bias,
+        o_weight,
+        final_gain,
+        jnp.asarray(near),
+        jnp.asarray(far),
+    )
     hidden, embedding = pl.pallas_call(
         functools.partial(kernel, n_seq, n_head),
-        out_shape=(
-            jax.ShapeDtypeStruct((rows, share), BF16),
-            jax.ShapeDtypeStruct((share,), F32),
-        ),
-        in_specs=[smem, hbm, vmem, hbm, vmem, hbm, vmem, hbm, vmem, hbm] + [vmem] * 5,
-        out_specs=(hbm, vmem),
+        out_shape=shapes,
+        in_specs=[hbm] * 13,
+        out_specs=(vmem, vmem),
         scratch_shapes=[
+            pltpu.SMEM((1,), jnp.int32),
+            pltpu.VMEM((width,), F32),
+            pltpu.VMEM((heads * HEAD_DIM,), F32),
+            pltpu.VMEM((HEAD_DIM,), F32),
+            pltpu.VMEM((HEAD_DIM,), F32),
+            pltpu.VMEM((share,), F32),
+            pltpu.VMEM(near.shape, F32),
+            pltpu.VMEM(far.shape[1:], F32),
             pltpu.VMEM((1, width), F32),
             pltpu.VMEM((1, heads * HEAD_DIM), F32),
             pltpu.VMEM((1, HEAD_DIM), F32),
@@ -540,11 +592,10 @@
             pltpu.VMEM((2, HEAD_DIM, heads * (rows // 2)), F32),
             pltpu.VMEM((rows, heads * HEAD_DIM), BF16),
             pltpu.VMEM((rows, share), F32),
-            pltpu.VMEM((rows, share), BF16),
             pltpu.VMEM((n_head, 8, rows), F32),
             pltpu.VMEM((n_seq, groups, HEAD_DIM), F32),
             pltpu.VMEM((n_head, 8, HEAD_DIM), F32),
-            dma((6,)),
+            dma((13,)),
             dma((4, half + 1)),
             dma((4, half + 1)),
             dma((len(chunks),)),
@@ -560,23 +611,17 @@
         ]
         + chunk_bufs,
         compiler_params=pltpu.CompilerParams(
-            collective_id=0, has_side_effects=True, vmem_limit_bytes=60 * 1024 * 1024
+            collective_id=0, has_side_effects=True, vmem_limit_bytes=48 * 1024 * 1024
         ),
-    )(
-        length,
-        tokens,
-        in_gain,
-        q_weight,
-        q_bias,
-        k_weight,
-        k_bias,
-        v_weight,
-        v_bias,
-        o_weight,
-        final_gain,
-        *tables,
-    )
-    return hidden, embedding
+    )(operands[0], *[pltpu.with_memory_space_constraint(x, pltpu.HBM) for x in operands[1:]])
+    return pl.pallas_call(
+        write_out,
+        out_shape=shapes,
+        in_specs=[vmem, vmem],
+        out_specs=(hbm, hbm),
+        scratch_shapes=[dma((2,))],
+        compiler_params=pltpu.CompilerParams(vmem_limit_bytes=2 * 1024 * 1024),
+    )(hidden, embedding)
 
 
 def solution(mesh):

time: 56.9 us -> 53.1 us (0.933)
  local copies, waits for them, and re-layouts: 3.09 us -> 0 us
  Pallas kernels: 52.3 us -> 51.5 us
    unnamed x2 -> x0, local copies, waits for them, and re-layouts: 3.09 us -> none
    pallas_call x1 -> x2, Pallas kernels: 52.3 us -> 51.5 us  [the longest x1 50.7 us: body(): pl.pallas_call(functools.partial(kernel, n_seq, n_head), out_shape=shapes...]
where the time goes in v1:
time: 53.1 us; the launch traced here: 52.9 us
  Pallas kernels  51.5 us (97%)
  between operations  1.45 us (3%)
    pallas_call x1, Pallas kernels, body(): pl.pallas_call(functools.partial(kernel, n_seq, n_head), out_shape=shapes...  50.7 us

profile of v1, /device:TPU:0, one launch (start us, length us, event | category | flops | bytes accessed | tf_op | source)
XLA Modules:
  0.0 52.9 jit_solution(6014409871914785308)
XLA Ops:
  1.3 50.7 %shard_map.140 = (bf16[256,896]{1,0:T(8,128)(2,1)S(1)}, f32[896]{0:T(1024)S(1)}) custom-call(s32[1]{0:T(128)S(6)} %copy.15.length_hbm, bf16[256,3584]{1,0:T(8,128)(2,1)} %tokens_hbm.1, f32[3584]{0:T(1024)} %gain_hbm.1, bf16[3584,896]{1,0:T(8,128)(2,1)} %wq_hbm.1, f32[896]{0:T(1024)} %qb_hbm.1, bf16[3584,128]{1,0:T(8,128)(2,1)} %wk_hbm.1, f32[128]{0:T(128)} %kb_hbm.1, ...), custom_call_target="tpu_custom_call" | custom-call | tf_op jit(solution)/shard_map/pallas_call | solution.py:561
  52.0 0.8 %shard_map.141 = (bf16[256,896]{1,0:T(8,128)(2,1)}, f32[896]{0:T(1024)}) custom-call(bf16[256,896]{1,0:T(8,128)(2,1)S(1)} %get-tuple-element.4.hidden_ref, f32[896]{0:T(1024)S(1)} %get-tuple-element.5.emb_ref), custom_call_target="tpu_custom_call" | custom-call | tf_op jit(solution)/shard_map/pallas_call | solution.py:617

commit v2 on v1

v2 whole, which is shorter than its diff:
```python
import functools

import jax
import jax.numpy as jnp
import numpy as np
from jax import lax
from jax.experimental import pallas as pl
from jax.experimental.pallas import tpu as pltpu
from jax.sharding import PartitionSpec as P

HEAD_DIM = 128
ROPE_BASE = 1000000.0
EPS = 1e-06
MESH = pl.DeviceIdType.MESH
F32 = jnp.float32
BF16 = jnp.bfloat16
LOW = -1e30


def widths(share):
    out, at = [], 0
    while at < share:
        width = 128 if at == 0 or share - at <= 256 else 256
        out.append((at, width))
        at += width
    return out


def dot(a, b):
    return jnp.dot(a, b, preferred_element_type=F32)


def kernel(
    n_seq,
    n_head,
    length_hbm,
    tokens_hbm,
    gain_hbm,
    wq_hbm,
    qb_hbm,
    wk_hbm,
    kb_hbm,
    wv_hbm,
    vb_hbm,
    wo_hbm,
    fgain_hbm,
    near_hbm,
    far_hbm,
    hid_bf,
    emb_ref,
    length_ref,
    gain_1d,
    qb_1d,
    kb_1d,
    vb_1d,
    fgain_1d,
    near,
    far,
    gain_ref,
    qb_ref,
    kb_ref,
    vb_ref,
    fgain_ref,
    tok,
    normed,
    wkv,
    wq,
    wo,
    cos,
    sin,
    qt,
    kbuf,
    vbuf,
    m_ref,
    acc_ref,
    att,
    hid,
    sqbuf,
    pbuf,
    wbuf,
    local_sem,
    ring_send,
    ring_recv,
    pair_send,
    pair_recv,
    cross_send,
    cross_recv,
    sq_send,
    sq_recv,
    pool_send,
    pool_recv,
    pow_send,
    pow_recv,
    *chunk_bufs,
):
    rows, width = tok.shape
    share = hid.shape[1]
    heads = qt.shape[1] // rows
    part_rows = rows // 2
    half = n_seq // 2
    n_y = n_head // 2
    chunks = widths(share)
    psend, precv = chunk_bufs[0::5], chunk_bufs[1::5]
    pown, ysend, yrecv = chunk_bufs[2::5], chunk_bufs[3::5], chunk_bufs[4::5]
    ms = lax.axis_index("seq")
    mh = lax.axis_index("head")

    def band(h):
        return pl.ds(h * part_rows, part_rows)

    tok_loads = [
        pltpu.make_async_copy(tokens_hbm.at[band(h)], tok.at[band(h)], local_sem.at[h])
        for h in (0, 1)
    ]
    kv_loads = [
        pltpu.make_async_copy(wk_hbm, wkv.at[:, :HEAD_DIM], local_sem.at[2]),
        pltpu.make_async_copy(wv_hbm, wkv.at[:, HEAD_DIM:], local_sem.at[3]),
    ]
    q_load = pltpu.make_async_copy(wq_hbm, wq, local_sem.at[4])
    o_load = pltpu.make_async_copy(wo_hbm, wo, local_sem.at[5])
    gain_load = pltpu.make_async_copy(gain_hbm, gain_1d, local_sem.at[6])
    smalls = [
        pltpu.make_async_copy(near_hbm, near, local_sem.at[7]),
        pltpu.make_async_copy(far_hbm.at[ms], far, local_sem.at[8]),
        pltpu.make_async_copy(kb_hbm, kb_1d, local_sem.at[9]),
        pltpu.make_async_copy(vb_hbm, vb_1d, local_sem.at[10]),
        pltpu.make_async_copy(qb_hbm, qb_1d, local_sem.at[11]),
        pltpu.make_async_copy(fgain_hbm, fgain_1d, local_sem.at[12]),
        pltpu.make_async_copy(length_hbm, length_ref, local_sem.at[13]),
    ]
    for load in [tok_loads[0], gain_load, *kv_loads, tok_loads[1], *smalls, q_load]:
        load.start()

    q2 = lax.div(ms, 2)
    pos = q2 + (ms - 2 * q2) * (n_seq - 1 - 2 * q2)

    def slot(p):
        p = lax.rem(p + 2 * n_seq, n_seq)
        back = lax.div(p, half)
        return (1 - back) * 2 * p + back * (2 * (n_seq - 1 - p) + 1)

    ends = (slot(pos + 1), slot(pos - 1))
    barrier = pltpu.get_barrier_semaphore()
    for end in ends:
        pl.semaphore_signal(barrier, inc=1, device_id={"seq": end}, device_id_type=MESH)
    for d in range(1, n_head):
        pl.semaphore_signal(
            barrier, inc=1, device_id={"head": lax.rem(mh + d, n_head)}, device_id_type=MESH
        )

    def spread(flat, row):
        for g in range(0, row.shape[1], HEAD_DIM):
            row[:, g : g + HEAD_DIM] = flat[g : g + HEAD_DIM].reshape(1, HEAD_DIM)

    m_ref[...] = jnp.full(m_ref.shape, LOW, F32)
    acc_ref[...] = jnp.zeros(acc_ref.shape, F32)
    ones = lax.broadcasted_iota(jnp.int32, (16, rows), 0)
    ones = jnp.where(ones == 0, 1.0, 0.0).astype(BF16)

    tok_loads[0].wait()
    gain_load.wait()
    spread(gain_1d, gain_ref)
    block = 16

    def norm_half(h):
        def step(i, carry):
            for k in (0, 1):
                at = pl.ds(pl.multiple_of(h * part_rows + (2 * i + k) * block, block), block)
                x = tok[at, :].astype(F32)
                mean = jnp.sum(x * x, axis=1, keepdims=True) / width
                normed[at, :] = (x * lax.rsqrt(mean + EPS) * gain_ref[...]).astype(BF16)
            return carry

        lax.fori_loop(0, part_rows // (2 * block), step, 0)

    def rope(u, h=None):
        at = slice(None) if h is None else band(h)
        return u * cos[at, :] + pltpu.roll(u, HEAD_DIM // 2, 1) * sin[at, :]

    def project(h):
        kv = dot(normed[band(h), :], wkv[...])
        kbuf[ms, band(h)] = rope(kv[:, :HEAD_DIM] + kb_ref[...], h).astype(BF16)
        vbuf[ms, h] = jnp.transpose(kv[:, HEAD_DIM:] + vb_ref[...]).astype(BF16)

    def moved(way, kind, h, s, hops):
        sign_of = 1 if way == 0 else -1
        at = slot(pos - sign_of * hops)
        part = vbuf.at[at, h] if kind else kbuf.at[at, band(h)]
        unit = 4 * way + 2 * kind + h
        return pltpu.make_async_remote_copy(
            src_ref=part,
            dst_ref=part,
            send_sem=ring_send.at[unit, s],
            recv_sem=ring_recv.at[unit, s],
            device_id={"seq": ends[way]},
            device_id_type=MESH,
        )

    def send(way, kind, h, s):
        return moved(way, kind, h, s, s - 1)

    def arrival(way, kind, h, s):
        return moved(way, kind, h, s, s)

    def send_own(h):
        for kind in (0, 1):
            for way in (0, 1):
                send(way, kind, h, 1).start()

    def forward(s, h, final):
        for kind in (0, 1):
            for way in (0, 1):
                arrival(way, kind, h, s).wait_recv()
                if not final or way == h:
                    send(way, kind, h, s + 1).start()

    norm_half(0)
    for small in smalls:
        small.wait()
    limit = length_ref[0]
    for flat, row in ((kb_1d, kb_ref), (vb_1d, vb_ref), (qb_1d, qb_ref), (fgain_1d, fgain_ref)):
        spread(flat, row)
    lane = lax.broadcasted_iota(jnp.int32, (1, HEAD_DIM), 1)
    sign = jnp.where(lane < HEAD_DIM // 2, -1.0, 1.0)
    co, so = far[0, :1], far[1, :1]
    cos[...] = near[0] * co - near[1] * so
    sin[...] = (near[1] * co + near[0] * so) * sign
    for load in kv_loads:
        load.wait()
    project(0)
    pl.semaphore_wait(barrier, n_head + 1)
    send_own(0)
    tok_loads[1].wait()
    norm_half(1)
    project(1)
    send_own(1)

    def put_query(h, u):
        u = rope(u + qb_ref[:, h * HEAD_DIM : (h + 1) * HEAD_DIM]) * HEAD_DIM ** (-0.5)
        qt[:, h * rows : (h + 1) * rows] = jnp.transpose(u).astype(BF16)

    def queries(first):
        last = min(first + 2, heads)
        u = dot(normed[...], wq[:, first * HEAD_DIM : last * HEAD_DIM])
        for h in range(first, last):
            put_query(h, u[:, (h - first) * HEAD_DIM : (h - first + 1) * HEAD_DIM])

    def attend(blocks, polls=()):
        row_at = lax.broadcasted_iota(jnp.int32, (rows, 1), 0)
        live = [b * rows + row_at < limit for b in blocks]
        polls = list(polls)

        def span(h):
            return slice(h * rows, (h + 1) * rows)

        def scores(h):
            return [jnp.where(ok, dot(kbuf[b], qt[:, span(h)]), LOW) for b, ok in zip(blocks, live)]

        def weigh(h, many):
            old = m_ref[:, span(h)][:1]
            top = functools.reduce(
                jnp.maximum, [jnp.max(s, axis=0, keepdims=True) for s in many], old
            )
            m_ref[:, span(h)] = jnp.broadcast_to(top, (8, rows))
            return h, jnp.exp(old - top), [jnp.exp(s - top).astype(BF16) for s in many]

        def mix(h, alpha, weights):
            new = None
            for b, p in zip(blocks, weights):
                v = jnp.concatenate([vbuf[b, 0], vbuf[b, 1]], axis=1)
                more = dot(jnp.concatenate([v, ones], axis=0), p)
                new = more if new is None else new + more
            acc_ref[:, span(h)] = acc_ref[:, span(h)] * alpha + new

        ready, held = scores(0), None
        for h in range(heads):
            after = scores(h + 1) if h + 1 < heads else None
            weighed = weigh(h, ready)
            if held is not None:
                mix(*held)
            held, ready = weighed, after
            if polls and polls[0][0] <= h:
                polls.pop(0)[1]()
        mix(*held)
        for _, poll in polls:
            poll()

    def polls(s, final):
        return [(1, lambda: forward(s, 0, final)), (4, lambda: forward(s, 1, final))]

    q_load.wait()
    o_load.start()
    queries(0)
    forward(1, 0, half == 2)
    queries(2)
    forward(1, 1, half == 2)
    for first in range(4, heads, 2):
        queries(first)
    attend([ms, slot(pos - 1), slot(pos + 1)], polls(2, half == 3))

    def ring_step(s, carry):
        attend([slot(pos - s), slot(pos + s)], polls(s + 1, False))
        return carry

    if half > 4:
        lax.fori_loop(2, half - 2, ring_step, 0)
    attend([slot(pos - half + 2), slot(pos + half - 2)], polls(half - 1, True))
    attend([slot(pos - half + 1), slot(pos + half - 1)])
    for way in (0, 1):
        for kind in (0, 1):
            arrival(way, kind, way, half).wait_recv()
    attend([slot(pos - half)])
    for h in range(heads):
        at = slice(h * rows, (h + 1) * rows)
        mixed = acc_ref[:HEAD_DIM, at] / acc_ref[HEAD_DIM : HEAD_DIM + 1, at]
        att[:, h * HEAD_DIM : (h + 1) * HEAD_DIM] = jnp.transpose(mixed).astype(BF16)

    o_load.wait()
    my = lax.div(mh, 2)
    mc = mh - 2 * my

    def far_y(d):
        return lax.rem(my + d, n_y)

    def partial(dest, at, wide):
        cols = pl.ds(pl.multiple_of(dest * share + at, HEAD_DIM), wide)
        return dot(att[...], wo[:, cols])

    def pair_copy(i, d):
        return pltpu.make_async_remote_copy(
            src_ref=psend[i].at[d],
            dst_ref=precv[i].at[d],
            send_sem=pair_send.at[i, d],
            recv_sem=pair_recv.at[i, d],
            device_id={"head": 2 * my + 1 - mc},
            device_id_type=MESH,
        )

    def cross_copy(i, d):
        return pltpu.make_async_remote_copy(
            src_ref=ysend[i].at[d - 1],
            dst_ref=yrecv[i].at[d - 1],
            send_sem=cross_send.at[i, d - 1],
            recv_sem=cross_recv.at[i, d - 1],
            device_id={"head": 2 * far_y(d) + mc},
            device_id_type=MESH,
        )

    def part_sums(i, d):
        at, wide = chunks[i]
        psend[i][d] = partial(2 * far_y(d) + 1 - mc, at, wide).astype(BF16)
        pair_copy(i, d).start()
        pown[i][d] = partial(2 * far_y(d) + mc, at, wide)

    def across(i):
        for d in range(1, n_y):
            pair_copy(i, d).wait_recv()
            ysend[i][d - 1] = (pown[i][d] + precv[i][d].astype(F32)).astype(BF16)
            cross_copy(i, d).start()

    for i in range(len(chunks)):
        for d in range(1, n_y):
            part_sums(i, d)
        if i:
            across(i - 1)
    across(len(chunks) - 1)
    for i in range(len(chunks)):
        part_sums(i, 0)

    squares = None
    for i, (at, wide) in enumerate(chunks):
        mine = pl.ds(pl.multiple_of(mh * share + at, HEAD_DIM), wide)
        pair_copy(i, 0).wait_recv()
        base = tok[:, mine].astype(F32) + (pown[i][0] + precv[i][0].astype(F32))
        for d in range(1, n_y):
            cross_copy(i, d).wait_recv()
            base = base + yrecv[i][d - 1].astype(F32)
        hid[:, at : at + wide] = base
        hid_bf[:, at : at + wide] = base.astype(BF16)
        for g in range(0, wide, HEAD_DIM):
            piece = base[:, g : g + HEAD_DIM]
            squares = piece * piece if squares is None else squares + piece * piece

    def head_copy(buf, send_sems, recv_sems, d):
        return pltpu.make_async_remote_copy(
            src_ref=buf.at[mh],
            dst_ref=buf.at[mh],
            send_sem=send_sems.at[d - 1],
            recv_sem=recv_sems.at[d - 1],
            device_id={"head": lax.rem(mh + d, n_head)},
            device_id_type=MESH,
        )

    def head_arrival(buf, send_sems, recv_sems, d):
        source = lax.rem(mh + n_head - d, n_head)
        return pltpu.make_async_remote_copy(
            src_ref=buf.at[source],
            dst_ref=buf.at[source],
            send_sem=send_sems.at[d - 1],
            recv_sem=recv_sems.at[d - 1],
            device_id={"head": source},
            device_id_type=MESH,
        )

    def head_sum(buf, send_sems, recv_sems, value):
        buf[mh] = jnp.broadcast_to(value, buf.shape[1:])
        for d in range(1, n_head):
            head_copy(buf, send_sems, recv_sems, d).start()
        for d in range(1, n_head):
            head_arrival(buf, send_sems, recv_sems, d).wait_recv()
        return functools.reduce(lambda a, b: a + b, [buf[d][:1] for d in range(n_head)])

    square_row = jnp.sum(jnp.transpose(squares), axis=0, keepdims=True)
    power = head_sum(sqbuf, sq_send, sq_recv, square_row)
    place = ms * rows + lax.broadcasted_iota(jnp.int32, (1, rows), 1)
    scale = jnp.where(place < limit, lax.rsqrt(power / width + EPS), 0.0)
    scale = jnp.transpose(jnp.broadcast_to(scale, (HEAD_DIM, rows)))

    groups = pbuf.shape[1]
    sums = []
    for g in range(0, share, HEAD_DIM):
        at = slice(g, g + HEAD_DIM)
        sums.append(jnp.sum(hid[:, at] * scale, axis=0, keepdims=True) * fgain_ref[:, at])
    sums += [jnp.zeros((1, HEAD_DIM), F32)] * (groups - len(sums))
    pbuf[ms] = jnp.concatenate(sums, axis=0)

    def pool_copy(d):
        return pltpu.make_async_remote_copy(
            src_ref=pbuf.at[ms],
            dst_ref=pbuf.at[ms],
            send_sem=pool_send.at[d - 1],
            recv_sem=pool_recv.at[d - 1],
            device_id={"seq": lax.rem(ms + d, n_seq)},
            device_id_type=MESH,
        )

    def pool_start(d, carry):
        pool_copy(d).start()
        return carry

    def pool_wait(d, carry):
        source = lax.rem(ms + n_seq - d, n_seq)
        pltpu.make_async_remote_copy(
            src_ref=pbuf.at[source],
            dst_ref=pbuf.at[source],
            send_sem=pool_send.at[d - 1],
            recv_sem=pool_recv.at[d - 1],
            device_id={"seq": source},
            device_id_type=MESH,
        ).wait_recv()
        return carry

    lax.fori_loop(1, n_seq, pool_start, 0)
    lax.fori_loop(1, n_seq, pool_wait, 0)
    mean = functools.reduce(lambda a, b: a + b, [pbuf[d] for d in range(n_seq)])
    mean = mean / limit.astype(F32)
    total = head_sum(wbuf, pow_send, pow_recv, jnp.sum(mean * mean, axis=0, keepdims=True))
    pooled = mean * lax.rsqrt(jnp.sum(total, axis=1, keepdims=True) / width + EPS)
    for g in range(share // HEAD_DIM):
        emb_ref[g * HEAD_DIM : (g + 1) * HEAD_DIM] = pooled[g : g + 1].reshape(HEAD_DIM)

    def sent(s, carry):
        for way in (0, 1):
            for kind in (0, 1):
                for h in (0, 1):
                    send(way, kind, h, s).wait_send()
        return carry

    lax.fori_loop(1, half, sent, 0)
    for way in (0, 1):
        for kind in (0, 1):
            send(way, kind, way, half).wait_send()
    for i in range(len(chunks)):
        for d in range(n_y):
            pair_copy(i, d).wait_send()
        for d in range(1, n_y):
            cross_copy(i, d).wait_send()
    for d in range(1, n_head):
        head_copy(sqbuf, sq_send, sq_recv, d).wait_send()
        head_copy(wbuf, pow_send, pow_recv, d).wait_send()

    def pool_sent(d, carry):
        pool_copy(d).wait_send()
        return carry

    lax.fori_loop(1, n_seq, pool_sent, 0)


def write_out(hidden_ref, emb_ref, hidden_hbm, emb_hbm, sems):
    copies = [
        pltpu.make_async_copy(hidden_ref, hidden_hbm, sems.at[0]),
        pltpu.make_async_copy(emb_ref, emb_hbm, sems.at[1]),
    ]
    for copy in copies:
        copy.start()
    for copy in copies:
        copy.wait()


def body(
    n_seq,
    n_head,
    tokens,
    length,
    in_gain,
    q_weight,
    q_bias,
    k_weight,
    k_bias,
    v_weight,
    v_bias,
    o_weight,
    final_gain,
):
    rows, width = tokens.shape
    share = width // n_head
    heads = q_weight.shape[1] // HEAD_DIM
    half = n_seq // 2
    n_y = n_head // 2
    inverse = ROPE_BASE ** (-(np.arange(HEAD_DIM // 2) * 2.0) / HEAD_DIM)
    inverse = np.concatenate([inverse, inverse])[None, :]
    near = np.arange(rows)[:, None] * inverse
    near = np.stack([np.cos(near), np.sin(near)]).astype(np.float32)
    far = (np.arange(n_seq) * rows)[:, None] * inverse
    far = np.stack([np.cos(far), np.sin(far)], axis=1).astype(np.float32)
    far = np.repeat(far[:, :, None, :], 8, axis=2)

    chunks = widths(share)
    groups = -(-share // (8 * HEAD_DIM)) * 8
    chunk_bufs = []
    for _, wide in chunks:
        chunk_bufs += [
            pltpu.VMEM((n_y, rows, wide), BF16),
            pltpu.VMEM((n_y, rows, wide), BF16),
            pltpu.VMEM((n_y, rows, wide), F32),
            pltpu.VMEM((n_y - 1, rows, wide), BF16),
            pltpu.VMEM((n_y - 1, rows, wide), BF16),
        ]
    dma = pltpu.SemaphoreType.DMA
    hbm = pl.BlockSpec(memory_space=pltpu.HBM)
    vmem = pl.BlockSpec(memory_space=pltpu.VMEM)
    shapes = (
        jax.ShapeDtypeStruct((rows, share), BF16),
        jax.ShapeDtypeStruct((share,), F32),
    )
    operands = (
        length,
        tokens,
        in_gain,
        q_weight,
        q_bias,
        k_weight,
        k_bias,
        v_weight,
        v_bias,
        o_weight,
        final_gain,
        jnp.asarray(near),
        jnp.asarray(far),
    )
    hidden, embedding = pl.pallas_call(
        functools.partial(kernel, n_seq, n_head),
        out_shape=shapes,
        in_specs=[hbm] * 13,
        out_specs=(vmem, vmem),
        scratch_shapes=[
            pltpu.SMEM((1,), jnp.int32),
            pltpu.VMEM((width,), F32),
            pltpu.VMEM((heads * HEAD_DIM,), F32),
            pltpu.VMEM((HEAD_DIM,), F32),
            pltpu.VMEM((HEAD_DIM,), F32),
            pltpu.VMEM((share,), F32),
            pltpu.VMEM(near.shape, F32),
            pltpu.VMEM(far.shape[1:], F32),
            pltpu.VMEM((1, width), F32),
            pltpu.VMEM((1, heads * HEAD_DIM), F32),
            pltpu.VMEM((1, HEAD_DIM), F32),
            pltpu.VMEM((1, HEAD_DIM), F32),
            pltpu.VMEM((1, share), F32),
            pltpu.VMEM((rows, width), BF16),
            pltpu.VMEM((rows, width), BF16),
            pltpu.VMEM((width, 2 * HEAD_DIM), BF16),
            pltpu.VMEM(q_weight.shape, BF16),
            pltpu.VMEM(o_weight.shape, BF16),
            pltpu.VMEM((rows, HEAD_DIM), F32),
            pltpu.VMEM((rows, HEAD_DIM), F32),
            pltpu.VMEM((HEAD_DIM, heads * rows), BF16),
            pltpu.VMEM((n_seq, rows, HEAD_DIM), BF16),
            pltpu.VMEM((n_seq, 2, HEAD_DIM, rows // 2), BF16),
            pltpu.VMEM((8, heads * rows), F32),
            pltpu.VMEM((HEAD_DIM + 16, heads * rows), F32),
            pltpu.VMEM((rows, heads * HEAD_DIM), BF16),
            pltpu.VMEM((rows, share), F32),
            pltpu.VMEM((n_head, 8, rows), F32),
            pltpu.VMEM((n_seq, groups, HEAD_DIM), F32),
            pltpu.VMEM((n_head, 8, HEAD_DIM), F32),
            dma((14,)),
            dma((8, half + 1)),
            dma((8, half + 1)),
            dma((len(chunks), n_y)),
            dma((len(chunks), n_y)),
            dma((len(chunks), n_y)),
            dma((len(chunks), n_y)),
            dma((n_head,)),
            dma((n_head,)),
            dma((n_seq,)),
            dma((n_seq,)),
            dma((n_head,)),
            dma((n_head,)),
        ]
        + chunk_bufs,
        compiler_params=pltpu.CompilerParams(
            collective_id=0, has_side_effects=True, vmem_limit_bytes=48 * 1024 * 1024
        ),
    )(operands[0], *[pltpu.with_memory_space_constraint(x, pltpu.HBM) for x in operands[1:]])
    return pl.pallas_call(
        write_out,
        out_shape=shapes,
        in_specs=[vmem, vmem],
        out_specs=(hbm, hbm),
        scratch_shapes=[dma((2,))],
        compiler_params=pltpu.CompilerParams(vmem_limit_bytes=2 * 1024 * 1024),
    )(hidden, embedding)


def solution(mesh):
    in_specs = (
        P("seq", None),
        P(),
        P(),
        P(None, "head"),
        P("head"),
        P(None, "head"),
        P("head"),
        P(None, "head"),
        P("head"),
        P("head", None),
        P("head"),
    )
    out_specs = (P("seq", "head"), P("head"))
    step = functools.partial(body, mesh.shape["seq"], mesh.shape["head"])
    return jax.shard_map(step, mesh=mesh, in_specs=in_specs, out_specs=out_specs, check_vma=False)
```

time: 53.1 us -> 49.3 us (0.928)
  Pallas kernels: 51.5 us -> 47.9 us
    pallas_call x1, Pallas kernels: 50.7 us -> 47.1 us  [body(): pl.pallas_call(functools.partial(kernel, n_seq, n_head), out_shape=shapes...]
where the time goes in v2:
time: 49.3 us; the launch traced here: 49.2 us
  Pallas kernels  47.9 us (97%)
  between operations  1.29 us (3%)
    pallas_call x1, Pallas kernels, body(): pl.pallas_call(functools.partial(kernel, n_seq, n_head), out_shape=shapes...  47.1 us

profile of v2, /device:TPU:0, one launch (start us, length us, event | category | flops | bytes accessed | tf_op | source)
XLA Modules:
  0.0 49.2 jit_solution(9423747599788623280)
XLA Ops:
  1.3 47.1 %shard_map.140 = (bf16[256,896]{1,0:T(8,128)(2,1)S(1)}, f32[896]{0:T(1024)S(1)}) custom-call(s32[1]{0:T(128)S(6)} %copy.15.length_hbm, bf16[256,3584]{1,0:T(8,128)(2,1)} %tokens_hbm.1, f32[3584]{0:T(1024)} %gain_hbm.1, bf16[3584,896]{1,0:T(8,128)(2,1)} %wq_hbm.1, f32[896]{0:T(1024)} %qb_hbm.1, bf16[3584,128]{1,0:T(8,128)(2,1)} %wk_hbm.1, f32[128]{0:T(128)} %kb_hbm.1, ...), custom_call_target="tpu_custom_call" | custom-call | tf_op jit(solution)/shard_map/pallas_call | solution.py:561
  48.4 0.8 %shard_map.141 = (bf16[256,896]{1,0:T(8,128)(2,1)}, f32[896]{0:T(1024)}) custom-call(bf16[256,896]{1,0:T(8,128)(2,1)S(1)} %get-tuple-element.4.hidden_ref, f32[896]{0:T(1024)S(1)} %get-tuple-element.5.emb_ref), custom_call_target="tpu_custom_call" | custom-call | tf_op jit(solution)/shard_map/pallas_call | solution.py:616

commit v3 on v2

v3 whole, which is shorter than its diff:
```python
import functools

import jax
import jax.numpy as jnp
import numpy as np
from jax import lax
from jax.experimental import pallas as pl
from jax.experimental.pallas import tpu as pltpu
from jax.sharding import PartitionSpec as P

HEAD_DIM = 128
ROPE_BASE = 1000000.0
EPS = 1e-06
MESH = pl.DeviceIdType.MESH
F32 = jnp.float32
BF16 = jnp.bfloat16
LOW = -1e30
SUBS = 1


def widths(share):
    out, at = [], 0
    while at < share:
        width = 128 if at == 0 or share - at <= 256 else 256
        out.append((at, width))
        at += width
    return out


def dot(a, b):
    return jnp.dot(a, b, preferred_element_type=F32)


def kernel(
    n_seq,
    n_head,
    length_hbm,
    tokens_hbm,
    gain_hbm,
    wq_hbm,
    qb_hbm,
    wk_hbm,
    kb_hbm,
    wv_hbm,
    vb_hbm,
    wo_hbm,
    fgain_hbm,
    near_hbm,
    far_hbm,
    hid_bf,
    emb_ref,
    length_ref,
    gain_1d,
    qb_1d,
    kb_1d,
    vb_1d,
    fgain_1d,
    near,
    far,
    gain_ref,
    qb_ref,
    kb_ref,
    vb_ref,
    fgain_ref,
    tok,
    normed,
    wkv,
    wq,
    wo,
    cos,
    sin,
    qt,
    kbuf,
    vbuf,
    m_ref,
    acc_ref,
    att,
    hid,
    psend,
    precv,
    pown,
    ysend,
    yrecv,
    sqbuf,
    pbuf,
    wbuf,
    local_sem,
    ring_send,
    ring_recv,
    pair_send,
    pair_recv,
    cross_send,
    cross_recv,
    sq_sem,
    pool_sem,
    pow_sem,
):
    rows, width = tok.shape
    share = hid.shape[1]
    heads = qt.shape[1] // rows
    part_rows = rows // 2
    half = n_seq // 2
    n_y = n_head // 2
    chunks = widths(share)
    ms = lax.axis_index("seq")
    mh = lax.axis_index("head")

    def band(h):
        return pl.ds(h * part_rows, part_rows)

    tok_loads = [
        pltpu.make_async_copy(tokens_hbm.at[band(h)], tok.at[band(h)], local_sem.at[h])
        for h in (0, 1)
    ]
    kv_loads = [
        pltpu.make_async_copy(wk_hbm, wkv.at[:, :HEAD_DIM], local_sem.at[2]),
        pltpu.make_async_copy(wv_hbm, wkv.at[:, HEAD_DIM:], local_sem.at[3]),
    ]
    q_load = pltpu.make_async_copy(wq_hbm, wq, local_sem.at[4])
    o_load = pltpu.make_async_copy(wo_hbm, wo, local_sem.at[5])
    gain_load = pltpu.make_async_copy(gain_hbm, gain_1d, local_sem.at[6])
    smalls = [
        pltpu.make_async_copy(near_hbm, near, local_sem.at[7]),
        pltpu.make_async_copy(far_hbm.at[ms], far, local_sem.at[8]),
        pltpu.make_async_copy(kb_hbm, kb_1d, local_sem.at[9]),
        pltpu.make_async_copy(vb_hbm, vb_1d, local_sem.at[10]),
        pltpu.make_async_copy(qb_hbm, qb_1d, local_sem.at[11]),
        pltpu.make_async_copy(fgain_hbm, fgain_1d, local_sem.at[12]),
        pltpu.make_async_copy(length_hbm, length_ref, local_sem.at[13]),
    ]
    for load in [tok_loads[0], gain_load, *kv_loads, tok_loads[1], *smalls, q_load]:
        load.start()

    q2 = lax.div(ms, 2)
    pos = q2 + (ms - 2 * q2) * (n_seq - 1 - 2 * q2)

    def slot(p):
        p = lax.rem(p + 2 * n_seq, n_seq)
        back = lax.div(p, half)
        return (1 - back) * 2 * p + back * (2 * (n_seq - 1 - p) + 1)

    ends = (slot(pos + 1), slot(pos - 1))
    barrier = pltpu.get_barrier_semaphore()
    for end in ends:
        pl.semaphore_signal(barrier, inc=1, device_id={"seq": end}, device_id_type=MESH)
    for d in range(1, n_head):
        pl.semaphore_signal(
            barrier, inc=1, device_id={"head": lax.rem(mh + d, n_head)}, device_id_type=MESH
        )

    def spread(flat, row):
        for g in range(0, row.shape[1], HEAD_DIM):
            row[:, g : g + HEAD_DIM] = flat[g : g + HEAD_DIM].reshape(1, HEAD_DIM)

    m_ref[...] = jnp.full(m_ref.shape, LOW, F32)
    acc_ref[...] = jnp.zeros(acc_ref.shape, F32)
    ones = lax.broadcasted_iota(jnp.int32, (16, rows), 0)
    ones = jnp.where(ones == 0, 1.0, 0.0).astype(BF16)

    tok_loads[0].wait()
    gain_load.wait()
    spread(gain_1d, gain_ref)
    block = 16

    def norm_half(h):
        def step(i, carry):
            for k in range(4):
                at = pl.ds(pl.multiple_of(h * part_rows + (4 * i + k) * block, block), block)
                x = tok[at, :].astype(F32)
                mean = jnp.sum(x * x, axis=1, keepdims=True) / width
                normed[at, :] = (x * lax.rsqrt(mean + EPS) * gain_ref[...]).astype(BF16)
            return carry

        lax.fori_loop(0, part_rows // (4 * block), step, 0)

    def rope(u, h=None):
        at = slice(None) if h is None else band(h)
        return u * cos[at, :] + pltpu.roll(u, HEAD_DIM // 2, 1) * sin[at, :]

    def project(h):
        mid = width // 512 * 256
        kv = dot(normed[band(h), :mid], wkv[:mid]) + dot(normed[band(h), mid:], wkv[mid:])
        kbuf[ms, band(h)] = rope(kv[:, :HEAD_DIM] + kb_ref[...], h).astype(BF16)
        vbuf[ms, h] = jnp.transpose(kv[:, HEAD_DIM:] + vb_ref[...]).astype(BF16)

    def moved(way, turn, sub, kind, s, hops):
        at = slot(pos - hops if way == 0 else pos + hops)
        first, count = (way ^ turn) * part_rows, part_rows // SUBS
        if kind:
            part = vbuf.at[at, way ^ turn, pl.ds(sub * (HEAD_DIM // SUBS), HEAD_DIM // SUBS)]
        else:
            part = kbuf.at[at, pl.ds(first + sub * count, count)]
        unit = (((s - 1) * 2 + turn) * 2 + way) * 2 * SUBS + sub * 2 + kind
        return pltpu.make_async_remote_copy(
            src_ref=part,
            dst_ref=part,
            send_sem=ring_send.at[kind],
            recv_sem=ring_recv.at[unit],
            device_id={"seq": ends[way]},
            device_id_type=MESH,
        )

    def send(way, turn, sub, kind, s):
        return moved(way, turn, sub, kind, s, s - 1)

    def arrival(way, turn, sub, kind, s):
        return moved(way, turn, sub, kind, s, s)

    def send_own(way, turn):
        for kind in (0, 1):
            for sub in range(SUBS):
                send(way, turn, sub, kind, 1).start()

    def forward(s, turn, go_on=True):
        for kind in (0, 1):
            for sub in range(SUBS):
                for way in (0, 1):
                    arrival(way, turn, sub, kind, s).wait_recv()
                    if go_on:
                        send(way, turn, sub, kind, s + 1).start()

    norm_half(0)
    tok_loads[1].wait()
    norm_half(1)
    for small in smalls:
        small.wait()
    limit = length_ref[0]
    for flat, row in ((kb_1d, kb_ref), (vb_1d, vb_ref), (qb_1d, qb_ref), (fgain_1d, fgain_ref)):
        spread(flat, row)
    lane = lax.broadcasted_iota(jnp.int32, (1, HEAD_DIM), 1)
    sign = jnp.where(lane < HEAD_DIM // 2, -1.0, 1.0)
    co, so = far[0, :1], far[1, :1]
    cos[...] = near[0] * co - near[1] * so
    sin[...] = (near[1] * co + near[0] * so) * sign
    for load in kv_loads:
        load.wait()
    project(0)
    pl.semaphore_wait(barrier, n_head + 1)
    send_own(0, 0)
    project(1)
    send_own(1, 0)
    send_own(0, 1)
    send_own(1, 1)

    def put_query(h, u):
        u = rope(u + qb_ref[:, h * HEAD_DIM : (h + 1) * HEAD_DIM]) * HEAD_DIM ** (-0.5)
        qt[:, h * rows : (h + 1) * rows] = jnp.transpose(u).astype(BF16)

    def queries(first):
        last = min(first + 4, heads)
        u = dot(normed[...], wq[:, first * HEAD_DIM : last * HEAD_DIM])
        for h in range(first, last):
            put_query(h, u[:, (h - first) * HEAD_DIM : (h - first + 1) * HEAD_DIM])

    def attend(blocks, poll=None, last=False):
        row_at = lax.broadcasted_iota(jnp.int32, (part_rows, 1), 0)
        live = [
            jnp.concatenate([b * rows + h * part_rows + row_at for b, h in block], axis=0) < limit
            for block in blocks
        ]

        def keys(block):
            parts = [kbuf[b, h * part_rows : (h + 1) * part_rows] for b, h in block]
            return jnp.concatenate(parts, axis=0)

        def values(block):
            return jnp.concatenate([vbuf[b, h] for b, h in block], axis=1)

        def span(h):
            return slice(h * rows, (h + 1) * rows)

        def scores(h):
            return [
                jnp.where(ok, dot(keys(block), qt[:, span(h)]), LOW)
                for block, ok in zip(blocks, live)
            ]

        def weigh(h, many):
            old = m_ref[:, span(h)][:1]
            top = functools.reduce(
                jnp.maximum, [jnp.max(s, axis=0, keepdims=True) for s in many], old
            )
            m_ref[:, span(h)] = jnp.broadcast_to(top, (8, rows))
            return h, jnp.exp(old - top), [jnp.exp(s - top).astype(BF16) for s in many]

        def mix(h, alpha, weights):
            new = None
            for block, p in zip(blocks, weights):
                more = dot(jnp.concatenate([values(block), ones], axis=0), p)
                new = more if new is None else new + more
            new = acc_ref[:, span(h)] * alpha + new
            if last:
                done = new[:HEAD_DIM] / new[HEAD_DIM : HEAD_DIM + 1]
                att[:, h * HEAD_DIM : (h + 1) * HEAD_DIM] = jnp.transpose(done).astype(BF16)
            else:
                acc_ref[:, span(h)] = new

        ready, held = scores(0), None
        for h in range(heads):
            after = scores(h + 1) if h + 1 < heads else None
            weighed = weigh(h, ready)
            if held is not None:
                mix(*held)
            held, ready = weighed, after
            if poll and h == heads // 2:
                poll()
        mix(*held)

    def whole(at):
        return ((at, 0), (at, 1))

    def pair(s):
        return [whole(slot(pos - s)), whole(slot(pos + s))]

    def cross_half(s, turn):
        return [((slot(pos - s), turn), (slot(pos + s), 1 - turn))]

    q_load.wait()
    o_load.start()
    for first in range(0, heads, 4):
        queries(first)
    forward(1, 0)
    attend([whole(ms)])
    forward(1, 1)

    def ring_step(s, carry):
        attend(pair(s), lambda: forward(s + 1, 0))
        forward(s + 1, 1)
        return carry

    if half > 4:
        lax.fori_loop(1, half - 3, ring_step, 0)
    ring_step(half - 3, 0)
    attend(pair(half - 2), lambda: forward(half - 1, 0))
    forward(half - 1, 1, False)
    attend(pair(half - 1))
    forward(half, 0, False)
    attend(cross_half(half, 0), last=True)
    o_load.wait()
    my = lax.div(mh, 2)
    mc = mh - 2 * my
    partner = {"head": 2 * my + 1 - mc}

    def far_y(d):
        return lax.rem(my + d, n_y)

    def partial(dest, at, wide):
        cols = pl.ds(pl.multiple_of(dest * share + at, HEAD_DIM), wide)
        return dot(att[...], wo[:, cols])

    def place(i):
        at, wide = chunks[i]
        return slice(at, at + wide)

    def pair_copy(i, d):
        return pltpu.make_async_remote_copy(
            src_ref=psend.at[d, :, place(i)],
            dst_ref=precv.at[d, :, place(i)],
            send_sem=pair_send.at[0],
            recv_sem=pair_recv.at[i, d],
            device_id=partner,
            device_id_type=MESH,
        )

    def cross_copy(i, d):
        return pltpu.make_async_remote_copy(
            src_ref=ysend.at[d - 1, :, place(i)],
            dst_ref=yrecv.at[d - 1, :, place(i)],
            send_sem=cross_send.at[0],
            recv_sem=cross_recv.at[i, d - 1],
            device_id={"head": 2 * far_y(d) + mc},
            device_id_type=MESH,
        )

    def part_sums(i, d):
        at, wide = chunks[i]
        psend[d, :, place(i)] = partial(2 * far_y(d) + 1 - mc, at, wide).astype(BF16)
        pair_copy(i, d).start()
        pown[d, :, place(i)] = partial(2 * far_y(d) + mc, at, wide)

    def across(i):
        for d in range(1, n_y):
            pair_copy(i, d).wait_recv()
            total = pown[d, :, place(i)] + precv[d, :, place(i)].astype(F32)
            ysend[d - 1, :, place(i)] = total.astype(BF16)
            cross_copy(i, d).start()

    @pl.when(mc == 0)
    def _():
        for i in range(len(chunks)):
            for d in range(1, n_y):
                part_sums(i, d)
            across(i)

    @pl.when(mc == 1)
    def _():
        for i in range(len(chunks)):
            for d in range(1, n_y):
                part_sums(i, d)
        for i in range(len(chunks)):
            across(i)

    for i in range(len(chunks)):
        part_sums(i, 0)

    squares = None
    for i, (at, wide) in enumerate(chunks):
        mine = pl.ds(pl.multiple_of(mh * share + at, HEAD_DIM), wide)
        pair_copy(i, 0).wait_recv()
        base = tok[:, mine].astype(F32) + (pown[0, :, place(i)] + precv[0, :, place(i)].astype(F32))
        for d in range(1, n_y):
            cross_copy(i, d).wait_recv()
            base = base + yrecv[d - 1, :, place(i)].astype(F32)
        hid[:, at : at + wide] = base
        hid_bf[:, at : at + wide] = base.astype(BF16)
        for g in range(0, wide, HEAD_DIM):
            piece = base[:, g : g + HEAD_DIM]
            squares = piece * piece if squares is None else squares + piece * piece

    def exchange(buf, axis, me, n, sems):
        def copy(d, slot_at):
            return pltpu.make_async_remote_copy(
                src_ref=buf.at[slot_at],
                dst_ref=buf.at[slot_at],
                send_sem=sems.at[0],
                recv_sem=sems.at[1],
                device_id={axis: lax.rem(me + d, n)},
                device_id_type=MESH,
            )

        for d in range(n - 1, 0, -1):
            copy(d, me).start()
        part = buf.at[pl.ds(0, n - 1)]
        pltpu.make_async_remote_copy(
            src_ref=part,
            dst_ref=part,
            send_sem=sems.at[0],
            recv_sem=sems.at[1],
            device_id=partner,
            device_id_type=MESH,
        ).wait_recv()

    def head_sum(buf, sems, value):
        buf[mh] = jnp.broadcast_to(value, buf.shape[1:])
        exchange(buf, "head", mh, n_head, sems)
        return functools.reduce(lambda a, b: a + b, [buf[d][:1] for d in range(n_head)])

    square_row = jnp.sum(jnp.transpose(squares), axis=0, keepdims=True)
    power = head_sum(sqbuf, sq_sem, square_row)
    where = ms * rows + lax.broadcasted_iota(jnp.int32, (1, rows), 1)
    scale = jnp.where(where < limit, lax.rsqrt(power / width + EPS), 0.0)
    scale = jnp.transpose(jnp.broadcast_to(scale, (HEAD_DIM, rows)))

    groups = pbuf.shape[1]
    sums = []
    for g in range(0, share, HEAD_DIM):
        at = slice(g, g + HEAD_DIM)
        sums.append(jnp.sum(hid[:, at] * scale, axis=0, keepdims=True) * fgain_ref[:, at])
    sums += [jnp.zeros((1, HEAD_DIM), F32)] * (groups - len(sums))
    pbuf[ms] = jnp.concatenate(sums, axis=0)

    exchange(pbuf, "seq", ms, n_seq, pool_sem)
    mean = functools.reduce(lambda a, b: a + b, [pbuf[d] for d in range(n_seq)])
    mean = mean / limit.astype(F32)
    total = head_sum(wbuf, pow_sem, jnp.sum(mean * mean, axis=0, keepdims=True))
    pooled = mean * lax.rsqrt(jnp.sum(total, axis=1, keepdims=True) / width + EPS)
    for g in range(share // HEAD_DIM):
        emb_ref[g * HEAD_DIM : (g + 1) * HEAD_DIM] = pooled[g : g + 1].reshape(HEAD_DIM)

    def all_sent(ref, sems, n):
        part = ref.at[pl.ds(0, n)]
        pltpu.make_async_remote_copy(
            src_ref=part,
            dst_ref=part,
            send_sem=sems.at[0],
            recv_sem=sems.at[0],
            device_id=partner,
            device_id_type=MESH,
        ).wait_send()

    all_sent(kbuf, ring_send.at[pl.ds(0, 1)], n_seq - 1)
    all_sent(vbuf, ring_send.at[pl.ds(1, 1)], n_seq - 1)
    all_sent(psend, pair_send, n_y)
    all_sent(ysend, cross_send, n_y - 1)
    all_sent(sqbuf, sq_sem, n_head - 1)
    all_sent(pbuf, pool_sem, n_seq - 1)
    all_sent(wbuf, pow_sem, n_head - 1)


def write_out(hidden_ref, emb_ref, hidden_hbm, emb_hbm, sems):
    copies = [
        pltpu.make_async_copy(hidden_ref, hidden_hbm, sems.at[0]),
        pltpu.make_async_copy(emb_ref, emb_hbm, sems.at[1]),
    ]
    for copy in copies:
        copy.start()
    for copy in copies:
        copy.wait()


def body(
    n_seq,
    n_head,
    tokens,
    length,
    in_gain,
    q_weight,
    q_bias,
    k_weight,
    k_bias,
    v_weight,
    v_bias,
    o_weight,
    final_gain,
):
    rows, width = tokens.shape
    share = width // n_head
    heads = q_weight.shape[1] // HEAD_DIM
    half = n_seq // 2
    n_y = n_head // 2
    inverse = ROPE_BASE ** (-(np.arange(HEAD_DIM // 2) * 2.0) / HEAD_DIM)
    inverse = np.concatenate([inverse, inverse])[None, :]
    near = np.arange(rows)[:, None] * inverse
    near = np.stack([np.cos(near), np.sin(near)]).astype(np.float32)
    far = (np.arange(n_seq) * rows)[:, None] * inverse
    far = np.stack([np.cos(far), np.sin(far)], axis=1).astype(np.float32)
    far = np.repeat(far[:, :, None, :], 8, axis=2)

    chunks = widths(share)
    groups = -(-share // (8 * HEAD_DIM)) * 8
    dma = pltpu.SemaphoreType.DMA
    hbm = pl.BlockSpec(memory_space=pltpu.HBM)
    vmem = pl.BlockSpec(memory_space=pltpu.VMEM)
    shapes = (
        jax.ShapeDtypeStruct((rows, share), BF16),
        jax.ShapeDtypeStruct((share,), F32),
    )
    operands = (
        length,
        tokens,
        in_gain,
        q_weight,
        q_bias,
        k_weight,
        k_bias,
        v_weight,
        v_bias,
        o_weight,
        final_gain,
        jnp.asarray(near),
        jnp.asarray(far),
    )
    hidden, embedding = pl.pallas_call(
        functools.partial(kernel, n_seq, n_head),
        out_shape=shapes,
        in_specs=[hbm] * 13,
        out_specs=(vmem, vmem),
        scratch_shapes=[
            pltpu.SMEM((1,), jnp.int32),
            pltpu.VMEM((width,), F32),
            pltpu.VMEM((heads * HEAD_DIM,), F32),
            pltpu.VMEM((HEAD_DIM,), F32),
            pltpu.VMEM((HEAD_DIM,), F32),
            pltpu.VMEM((share,), F32),
            pltpu.VMEM(near.shape, F32),
            pltpu.VMEM(far.shape[1:], F32),
            pltpu.VMEM((1, width), F32),
            pltpu.VMEM((1, heads * HEAD_DIM), F32),
            pltpu.VMEM((1, HEAD_DIM), F32),
            pltpu.VMEM((1, HEAD_DIM), F32),
            pltpu.VMEM((1, share), F32),
            pltpu.VMEM((rows, width), BF16),
            pltpu.VMEM((rows, width), BF16),
            pltpu.VMEM((width, 2 * HEAD_DIM), BF16),
            pltpu.VMEM(q_weight.shape, BF16),
            pltpu.VMEM(o_weight.shape, BF16),
            pltpu.VMEM((rows, HEAD_DIM), F32),
            pltpu.VMEM((rows, HEAD_DIM), F32),
            pltpu.VMEM((HEAD_DIM, heads * rows), BF16),
            pltpu.VMEM((n_seq, rows, HEAD_DIM), BF16),
            pltpu.VMEM((n_seq, 2, HEAD_DIM, rows // 2), BF16),
            pltpu.VMEM((8, heads * rows), F32),
            pltpu.VMEM((HEAD_DIM + 16, heads * rows), F32),
            pltpu.VMEM((rows, heads * HEAD_DIM), BF16),
            pltpu.VMEM((rows, share), F32),
            pltpu.VMEM((n_y, rows, share), BF16),
            pltpu.VMEM((n_y, rows, share), BF16),
            pltpu.VMEM((n_y, rows, share), F32),
            pltpu.VMEM((n_y - 1, rows, share), BF16),
            pltpu.VMEM((n_y - 1, rows, share), BF16),
            pltpu.VMEM((n_head, 8, rows), F32),
            pltpu.VMEM((n_seq, groups, HEAD_DIM), F32),
            pltpu.VMEM((n_head, 8, HEAD_DIM), F32),
            dma((14,)),
            dma((2,)),
            dma((SUBS * (8 * half - 4),)),
            dma((1,)),
            dma((len(chunks), n_y)),
            dma((1,)),
            dma((len(chunks), n_y - 1)),
            dma((2,)),
            dma((2,)),
            dma((2,)),
        ],
        compiler_params=pltpu.CompilerParams(
            collective_id=0, has_side_effects=True, vmem_limit_bytes=48 * 1024 * 1024
        ),
    )(operands[0], *[pltpu.with_memory_space_constraint(x, pltpu.HBM) for x in operands[1:]])
    return pl.pallas_call(
        write_out,
        out_shape=shapes,
        in_specs=[vmem, vmem],
        out_specs=(hbm, hbm),
        scratch_shapes=[dma((2,))],
        compiler_params=pltpu.CompilerParams(vmem_limit_bytes=2 * 1024 * 1024),
    )(hidden, embedding)


def solution(mesh):
    in_specs = (
        P("seq", None),
        P(),
        P(),
        P(None, "head"),
        P("head"),
        P(None, "head"),
        P("head"),
        P(None, "head"),
        P("head"),
        P("head", None),
        P("head"),
    )
    out_specs = (P("seq", "head"), P("head"))
    step = functools.partial(body, mesh.shape["seq"], mesh.shape["head"])
    return jax.shard_map(step, mesh=mesh, in_specs=in_specs, out_specs=out_specs, check_vma=False)
```

time: 49.3 us -> 47.7 us (0.968)
  Pallas kernels: 47.9 us -> 46.1 us
    pallas_call x1, Pallas kernels: 47.1 us -> 45.3 us  [body(): pl.pallas_call(functools.partial(kernel, n_seq, n_head), out_shape=shapes...]
where the time goes in v3:
time: 47.7 us; the launch traced here: 47.5 us
  Pallas kernels  46.1 us (97%)
  between operations  1.45 us (3%)
    pallas_call x1, Pallas kernels, body(): pl.pallas_call(functools.partial(kernel, n_seq, n_head), out_shape=shapes...  45.3 us

profile of v3, /device:TPU:0, one launch (start us, length us, event | category | flops | bytes accessed | tf_op | source)
XLA Modules:
  0.0 47.5 jit_solution(9186661352752064207)
XLA Ops:
  1.3 45.3 %shard_map.140 = (bf16[256,896]{1,0:T(8,128)(2,1)S(1)}, f32[896]{0:T(1024)S(1)}) custom-call(s32[1]{0:T(128)S(6)} %copy.15.length_hbm, bf16[256,3584]{1,0:T(8,128)(2,1)} %tokens_hbm.1, f32[3584]{0:T(1024)} %gain_hbm.1, bf16[3584,896]{1,0:T(8,128)(2,1)} %wq_hbm.1, f32[896]{0:T(1024)} %qb_hbm.1, bf16[3584,128]{1,0:T(8,128)(2,1)} %wk_hbm.1, f32[128]{0:T(128)} %kb_hbm.1, ...), custom_call_target="tpu_custom_call" | custom-call | tf_op jit(solution)/shard_map/pallas_call | solution.py:553
  46.6 0.8 %shard_map.141 = (bf16[256,896]{1,0:T(8,128)(2,1)}, f32[896]{0:T(1024)}) custom-call(bf16[256,896]{1,0:T(8,128)(2,1)S(1)} %get-tuple-element.4.hidden_ref, f32[896]{0:T(1024)S(1)} %get-tuple-element.5.emb_ref), custom_call_target="tpu_custom_call" | custom-call | tf_op jit(solution)/shard_map/pallas_call | solution.py:609

commit v4 on v3

--- a/solution.py
+++ b/solution.py
@@ -16,6 +16,7 @@
 BF16 = jnp.bfloat16
 LOW = -1e30
 SUBS = 1
+GROUP = 4
 
 
 def widths(share):
@@ -128,7 +129,7 @@
         pltpu.make_async_copy(fgain_hbm, fgain_1d, local_sem.at[12]),
         pltpu.make_async_copy(length_hbm, length_ref, local_sem.at[13]),
     ]
-    for load in [tok_loads[0], gain_load, *kv_loads, tok_loads[1], *smalls, q_load]:
+    for load in [tok_loads[0], gain_load, tok_loads[1], *kv_loads, *smalls, q_load]:
         load.start()
 
     q2 = lax.div(ms, 2)
@@ -140,6 +141,9 @@
         return (1 - back) * 2 * p + back * (2 * (n_seq - 1 - p) + 1)
 
     ends = (slot(pos + 1), slot(pos - 1))
+    my = lax.div(mh, 2)
+    mc = mh - 2 * my
+    partner = {"head": 2 * my + 1 - mc}
     barrier = pltpu.get_barrier_semaphore()
     for end in ends:
         pl.semaphore_signal(barrier, inc=1, device_id={"seq": end}, device_id_type=MESH)
@@ -181,7 +185,7 @@
         mid = width // 512 * 256
         kv = dot(normed[band(h), :mid], wkv[:mid]) + dot(normed[band(h), mid:], wkv[mid:])
         kbuf[ms, band(h)] = rope(kv[:, :HEAD_DIM] + kb_ref[...], h).astype(BF16)
-        vbuf[ms, h] = jnp.transpose(kv[:, HEAD_DIM:] + vb_ref[...]).astype(BF16)
+        vbuf[ms, h] = jnp.transpose((kv[:, HEAD_DIM:] + vb_ref[...]).astype(BF16))
 
     def moved(way, turn, sub, kind, s, hops):
         at = slot(pos - hops if way == 0 else pos + hops)
@@ -236,15 +240,22 @@
         load.wait()
     project(0)
     pl.semaphore_wait(barrier, n_head + 1)
-    send_own(0, 0)
+
+    @pl.when(mc == 0)
+    def _():
+        send_own(0, 0)
+
     project(1)
-    send_own(1, 0)
-    send_own(0, 1)
-    send_own(1, 1)
+
+    @pl.when(mc == 0)
+    def _():
+        send_own(1, 0)
+        send_own(0, 1)
+        send_own(1, 1)
 
     def put_query(h, u):
         u = rope(u + qb_ref[:, h * HEAD_DIM : (h + 1) * HEAD_DIM]) * HEAD_DIM ** (-0.5)
-        qt[:, h * rows : (h + 1) * rows] = jnp.transpose(u).astype(BF16)
+        qt[:, h * rows : (h + 1) * rows] = jnp.transpose(u.astype(BF16))
 
     def queries(first):
         last = min(first + 4, heads)
@@ -252,7 +263,7 @@
         for h in range(first, last):
             put_query(h, u[:, (h - first) * HEAD_DIM : (h - first + 1) * HEAD_DIM])
 
-    def attend(blocks, poll=None, last=False):
+    def attend(blocks, poll=None, last=False, group=1):
         row_at = lax.broadcasted_iota(jnp.int32, (part_rows, 1), 0)
         live = [
             jnp.concatenate([b * rows + h * part_rows + row_at for b, h in block], axis=0) < limit
@@ -267,7 +278,7 @@
             return jnp.concatenate([vbuf[b, h] for b, h in block], axis=1)
 
         def span(h):
-            return slice(h * rows, (h + 1) * rows)
+            return slice(h * rows, min(h + group, heads) * rows)
 
         def scores(h):
             return [
@@ -280,7 +291,7 @@
             top = functools.reduce(
                 jnp.maximum, [jnp.max(s, axis=0, keepdims=True) for s in many], old
             )
-            m_ref[:, span(h)] = jnp.broadcast_to(top, (8, rows))
+            m_ref[:, span(h)] = jnp.broadcast_to(top, (8, top.shape[1]))
             return h, jnp.exp(old - top), [jnp.exp(s - top).astype(BF16) for s in many]
 
         def mix(h, alpha, weights):
@@ -290,14 +301,16 @@
                 new = more if new is None else new + more
             new = acc_ref[:, span(h)] * alpha + new
             if last:
-                done = new[:HEAD_DIM] / new[HEAD_DIM : HEAD_DIM + 1]
-                att[:, h * HEAD_DIM : (h + 1) * HEAD_DIM] = jnp.transpose(done).astype(BF16)
+                done = (new[:HEAD_DIM] / new[HEAD_DIM : HEAD_DIM + 1]).astype(BF16)
+                for g in range(done.shape[1] // rows):
+                    at = slice((h + g) * HEAD_DIM, (h + g + 1) * HEAD_DIM)
+                    att[:, at] = jnp.transpose(done[:, g * rows : (g + 1) * rows])
             else:
                 acc_ref[:, span(h)] = new
 
         ready, held = scores(0), None
-        for h in range(heads):
-            after = scores(h + 1) if h + 1 < heads else None
+        for h in range(0, heads, group):
+            after = scores(h + group) if h + group < heads else None
             weighed = weigh(h, ready)
             if held is not None:
                 mix(*held)
@@ -317,10 +330,18 @@
 
     q_load.wait()
     o_load.start()
-    for first in range(0, heads, 4):
+    queries(0)
+
+    @pl.when(mc == 1)
+    def _():
+        for turn in (0, 1):
+            for way in (0, 1):
+                send_own(way, turn)
+
+    for first in range(4, heads, 4):
         queries(first)
     forward(1, 0)
-    attend([whole(ms)])
+    attend([whole(ms)], group=GROUP)
     forward(1, 1)
 
     def ring_step(s, carry):
@@ -335,11 +356,8 @@
     forward(half - 1, 1, False)
     attend(pair(half - 1))
     forward(half, 0, False)
-    attend(cross_half(half, 0), last=True)
+    attend(cross_half(half, 0), last=True, group=GROUP)
     o_load.wait()
-    my = lax.div(mh, 2)
-    mc = mh - 2 * my
-    partner = {"head": 2 * my + 1 - mc}
 
     def far_y(d):
         return lax.rem(my + d, n_y)

time: 47.7 us -> 47.2 us (0.990)
  Pallas kernels: 46.1 us -> 45.6 us
where the time goes in v4:
time: 47.2 us; the launch traced here: 47.1 us
  Pallas kernels  45.6 us (97%)
  between operations  1.45 us (3%)
    pallas_call x1, Pallas kernels, body(): pl.pallas_call(functools.partial(kernel, n_seq, n_head), out_shape=shapes...  44.8 us

profile of v4, /device:TPU:0, one launch (start us, length us, event | category | flops | bytes accessed | tf_op | source)
XLA Modules:
  0.0 47.1 jit_solution(51149912952818746)
XLA Ops:
  1.3 44.8 %shard_map.140 = (bf16[256,896]{1,0:T(8,128)(2,1)S(1)}, f32[896]{0:T(1024)S(1)}) custom-call(s32[1]{0:T(128)S(6)} %copy.15.length_hbm, bf16[256,3584]{1,0:T(8,128)(2,1)} %tokens_hbm.1, f32[3584]{0:T(1024)} %gain_hbm.1, bf16[3584,896]{1,0:T(8,128)(2,1)} %wq_hbm.1, f32[896]{0:T(1024)} %qb_hbm.1, bf16[3584,128]{1,0:T(8,128)(2,1)} %wk_hbm.1, f32[128]{0:T(128)} %kb_hbm.1, ...), custom_call_target="tpu_custom_call" | custom-call | tf_op jit(solution)/shard_map/pallas_call | solution.py:571
  46.1 0.8 %shard_map.141 = (bf16[256,896]{1,0:T(8,128)(2,1)}, f32[896]{0:T(1024)}) custom-call(bf16[256,896]{1,0:T(8,128)(2,1)S(1)} %get-tuple-element.4.hidden_ref, f32[896]{0:T(1024)S(1)} %get-tuple-element.5.emb_ref), custom_call_target="tpu_custom_call" | custom-call | tf_op jit(solution)/shard_map/pallas_call | solution.py:627

commit v5 on v4

--- a/solution.py
+++ b/solution.py
@@ -85,6 +85,8 @@
     sqbuf,
     pbuf,
     wbuf,
+    shared,
+    other,
     local_sem,
     ring_send,
     ring_recv,
@@ -95,6 +97,7 @@
     sq_sem,
     pool_sem,
     pow_sem,
+    share_sem,
 ):
     rows, width = tok.shape
     share = hid.shape[1]
@@ -109,27 +112,30 @@
     def band(h):
         return pl.ds(h * part_rows, part_rows)
 
+    def quarter(i):
+        return pl.ds(i * (rows // 4), rows // 4)
+
     tok_loads = [
-        pltpu.make_async_copy(tokens_hbm.at[band(h)], tok.at[band(h)], local_sem.at[h])
-        for h in (0, 1)
+        pltpu.make_async_copy(tokens_hbm.at[quarter(i)], tok.at[quarter(i)], local_sem.at[i])
+        for i in range(4)
     ]
     kv_loads = [
-        pltpu.make_async_copy(wk_hbm, wkv.at[:, :HEAD_DIM], local_sem.at[2]),
-        pltpu.make_async_copy(wv_hbm, wkv.at[:, HEAD_DIM:], local_sem.at[3]),
+        pltpu.make_async_copy(wk_hbm, wkv.at[:, :HEAD_DIM], local_sem.at[4]),
+        pltpu.make_async_copy(wv_hbm, wkv.at[:, HEAD_DIM:], local_sem.at[5]),
     ]
-    q_load = pltpu.make_async_copy(wq_hbm, wq, local_sem.at[4])
-    o_load = pltpu.make_async_copy(wo_hbm, wo, local_sem.at[5])
-    gain_load = pltpu.make_async_copy(gain_hbm, gain_1d, local_sem.at[6])
+    q_load = pltpu.make_async_copy(wq_hbm, wq, local_sem.at[6])
+    o_load = pltpu.make_async_copy(wo_hbm, wo, local_sem.at[7])
+    gain_load = pltpu.make_async_copy(gain_hbm, gain_1d, local_sem.at[8])
     smalls = [
-        pltpu.make_async_copy(near_hbm, near, local_sem.at[7]),
-        pltpu.make_async_copy(far_hbm.at[ms], far, local_sem.at[8]),
-        pltpu.make_async_copy(kb_hbm, kb_1d, local_sem.at[9]),
-        pltpu.make_async_copy(vb_hbm, vb_1d, local_sem.at[10]),
-        pltpu.make_async_copy(qb_hbm, qb_1d, local_sem.at[11]),
-        pltpu.make_async_copy(fgain_hbm, fgain_1d, local_sem.at[12]),
-        pltpu.make_async_copy(length_hbm, length_ref, local_sem.at[13]),
+        pltpu.make_async_copy(near_hbm, near, local_sem.at[9]),
+        pltpu.make_async_copy(far_hbm.at[ms], far, local_sem.at[10]),
+        pltpu.make_async_copy(kb_hbm, kb_1d, local_sem.at[11]),
+        pltpu.make_async_copy(vb_hbm, vb_1d, local_sem.at[12]),
+        pltpu.make_async_copy(qb_hbm, qb_1d, local_sem.at[13]),
+        pltpu.make_async_copy(fgain_hbm, fgain_1d, local_sem.at[14]),
+        pltpu.make_async_copy(length_hbm, length_ref, local_sem.at[15]),
     ]
-    for load in [tok_loads[0], gain_load, tok_loads[1], *kv_loads, *smalls, q_load]:
+    for load in [tok_loads[0], gain_load, *tok_loads[1:], *kv_loads, *smalls, q_load]:
         load.start()
 
     q2 = lax.div(ms, 2)
@@ -161,29 +167,23 @@
     ones = lax.broadcasted_iota(jnp.int32, (16, rows), 0)
     ones = jnp.where(ones == 0, 1.0, 0.0).astype(BF16)
 
-    tok_loads[0].wait()
     gain_load.wait()
     spread(gain_1d, gain_ref)
     block = 16
 
-    def norm_half(h):
-        def step(i, carry):
-            for k in range(4):
-                at = pl.ds(pl.multiple_of(h * part_rows + (4 * i + k) * block, block), block)
-                x = tok[at, :].astype(F32)
-                mean = jnp.sum(x * x, axis=1, keepdims=True) / width
-                normed[at, :] = (x * lax.rsqrt(mean + EPS) * gain_ref[...]).astype(BF16)
-            return carry
-
-        lax.fori_loop(0, part_rows // (4 * block), step, 0)
+    def norm_quarter(q):
+        for k in range(rows // 4 // block):
+            at = pl.ds(q * (rows // 4) + k * block, block)
+            x = tok[at, :].astype(F32)
+            mean = jnp.sum(x * x, axis=1, keepdims=True) / width
+            normed[at, :] = (x * lax.rsqrt(mean + EPS) * gain_ref[...]).astype(BF16)
 
     def rope(u, h=None):
         at = slice(None) if h is None else band(h)
         return u * cos[at, :] + pltpu.roll(u, HEAD_DIM // 2, 1) * sin[at, :]
 
     def project(h):
-        mid = width // 512 * 256
-        kv = dot(normed[band(h), :mid], wkv[:mid]) + dot(normed[band(h), mid:], wkv[mid:])
+        kv = dot(normed[band(h), :], wkv[...])
         kbuf[ms, band(h)] = rope(kv[:, :HEAD_DIM] + kb_ref[...], h).astype(BF16)
         vbuf[ms, h] = jnp.transpose((kv[:, HEAD_DIM:] + vb_ref[...]).astype(BF16))
 
@@ -215,17 +215,21 @@
             for sub in range(SUBS):
                 send(way, turn, sub, kind, 1).start()
 
-    def forward(s, turn, go_on=True):
+    def arrive(s, turn, kind):
+        for sub in range(SUBS):
+            for way in (0, 1):
+                arrival(way, turn, sub, kind, s).wait_recv()
+
+    def forward(s, turn):
         for kind in (0, 1):
             for sub in range(SUBS):
                 for way in (0, 1):
                     arrival(way, turn, sub, kind, s).wait_recv()
-                    if go_on:
-                        send(way, turn, sub, kind, s + 1).start()
-
-    norm_half(0)
-    tok_loads[1].wait()
-    norm_half(1)
+                    send(way, turn, sub, kind, s + 1).start()
+
+    for q in range(4):
+        tok_loads[q].wait()
+        norm_quarter(q)
     for small in smalls:
         small.wait()
     limit = length_ref[0]
@@ -263,7 +267,7 @@
         for h in range(first, last):
             put_query(h, u[:, (h - first) * HEAD_DIM : (h - first + 1) * HEAD_DIM])
 
-    def attend(blocks, poll=None, last=False, group=1):
+    def attend(blocks, poll=None, last=False, group=1, values_in=None):
         row_at = lax.broadcasted_iota(jnp.int32, (part_rows, 1), 0)
         live = [
             jnp.concatenate([b * rows + h * part_rows + row_at for b, h in block], axis=0) < limit
@@ -312,6 +316,8 @@
         for h in range(0, heads, group):
             after = scores(h + group) if h + group < heads else None
             weighed = weigh(h, ready)
+            if h == 0 and values_in:
+                values_in()
             if held is not None:
                 mix(*held)
             held, ready = weighed, after
@@ -353,10 +359,12 @@
         lax.fori_loop(1, half - 3, ring_step, 0)
     ring_step(half - 3, 0)
     attend(pair(half - 2), lambda: forward(half - 1, 0))
-    forward(half - 1, 1, False)
-    attend(pair(half - 1))
-    forward(half, 0, False)
-    attend(cross_half(half, 0), last=True, group=GROUP)
+    arrive(half - 1, 1, 0)
+    attend(pair(half - 1), values_in=lambda: arrive(half - 1, 1, 1))
+    arrive(half, 0, 0)
+    attend(
+        cross_half(half, 0), last=True, group=GROUP, values_in=lambda: arrive(half, 0, 1)
+    )
     o_load.wait()
 
     def far_y(d):
@@ -477,10 +485,62 @@
     sums += [jnp.zeros((1, HEAD_DIM), F32)] * (groups - len(sums))
     pbuf[ms] = jnp.concatenate(sums, axis=0)
 
+    shared[...] = pbuf[ms].astype(BF16)
+
+    def share_copy(d):
+        return pltpu.make_async_remote_copy(
+            src_ref=shared,
+            dst_ref=other.at[ms],
+            send_sem=share_sem.at[0],
+            recv_sem=share_sem.at[1],
+            device_id={"seq": lax.rem(ms + d, n_seq), **partner},
+            device_id_type=MESH,
+        )
+
+    for d in range(n_seq - 1, -1, -1):
+        share_copy(d).start()
     exchange(pbuf, "seq", ms, n_seq, pool_sem)
+    every_share = pltpu.make_async_remote_copy(
+        src_ref=other,
+        dst_ref=other,
+        send_sem=share_sem.at[0],
+        recv_sem=share_sem.at[1],
+        device_id=partner,
+        device_id_type=MESH,
+    )
+    every_share.wait_recv()
     mean = functools.reduce(lambda a, b: a + b, [pbuf[d] for d in range(n_seq)])
     mean = mean / limit.astype(F32)
-    total = head_sum(wbuf, pow_sem, jnp.sum(mean * mean, axis=0, keepdims=True))
+    near_mean = functools.reduce(
+        lambda a, b: a + b, [other[d].astype(F32) for d in range(n_seq)]
+    )
+    near_mean = near_mean / limit.astype(F32)
+    power = jnp.sum(mean * mean + near_mean * near_mean, axis=0, keepdims=True)
+    wbuf[my] = jnp.broadcast_to(power, wbuf.shape[1:])
+
+    @pl.when(mc == 1)
+    def _():
+        for d in range(1, n_y):
+            for c in (0, 1):
+                pltpu.make_async_remote_copy(
+                    src_ref=wbuf.at[my],
+                    dst_ref=wbuf.at[my],
+                    send_sem=pow_sem.at[0],
+                    recv_sem=pow_sem.at[1],
+                    device_id={"head": 2 * far_y(d) + c},
+                    device_id_type=MESH,
+                ).start()
+
+    part = wbuf.at[pl.ds(0, n_y - 1)]
+    pltpu.make_async_remote_copy(
+        src_ref=part,
+        dst_ref=part,
+        send_sem=pow_sem.at[0],
+        recv_sem=pow_sem.at[1],
+        device_id=partner,
+        device_id_type=MESH,
+    ).wait_recv()
+    total = functools.reduce(lambda a, b: a + b, [wbuf[y][:1] for y in range(n_y)])
     pooled = mean * lax.rsqrt(jnp.sum(total, axis=1, keepdims=True) / width + EPS)
     for g in range(share // HEAD_DIM):
         emb_ref[g * HEAD_DIM : (g + 1) * HEAD_DIM] = pooled[g : g + 1].reshape(HEAD_DIM)
@@ -502,7 +562,11 @@
     all_sent(ysend, cross_send, n_y - 1)
     all_sent(sqbuf, sq_sem, n_head - 1)
     all_sent(pbuf, pool_sem, n_seq - 1)
-    all_sent(wbuf, pow_sem, n_head - 1)
+    every_share.wait_send()
+
+    @pl.when(mc == 1)
+    def _():
+        all_sent(wbuf, pow_sem, 2 * (n_y - 1))
 
 
 def write_out(hidden_ref, emb_ref, hidden_hbm, emb_hbm, sems):
@@ -609,13 +673,16 @@
             pltpu.VMEM((n_head, 8, rows), F32),
             pltpu.VMEM((n_seq, groups, HEAD_DIM), F32),
             pltpu.VMEM((n_head, 8, HEAD_DIM), F32),
-            dma((14,)),
+            pltpu.VMEM((groups, HEAD_DIM), BF16),
+            pltpu.VMEM((n_seq, groups, HEAD_DIM), BF16),
+            dma((16,)),
             dma((2,)),
             dma((SUBS * (8 * half - 4),)),
             dma((1,)),
             dma((len(chunks), n_y)),
             dma((1,)),
             dma((len(chunks), n_y - 1)),
+            dma((2,)),
             dma((2,)),
             dma((2,)),
             dma((2,)),

time: 47.2 us -> 46.1 us (0.977)
  Pallas kernels: 45.6 us -> 44.5 us
    pallas_call x1, Pallas kernels: 44.8 us -> 43.7 us  [body(): pl.pallas_call(functools.partial(kernel, n_seq, n_head), out_shape=shapes...]
where the time goes in v5:
time: 46.1 us; the launch traced here: 46 us
  Pallas kernels  44.5 us (97%)
  between operations  1.45 us (3%)
    pallas_call x1, Pallas kernels, body(): pl.pallas_call(functools.partial(kernel, n_seq, n_head), out_shape=shapes...  43.7 us

profile of v5, /device:TPU:0, one launch (start us, length us, event | category | flops | bytes accessed | tf_op | source)
XLA Modules:
  0.0 46.0 jit_solution(8102383282336959865)
XLA Ops:
  1.3 43.7 %shard_map.140 = (bf16[256,896]{1,0:T(8,128)(2,1)S(1)}, f32[896]{0:T(1024)S(1)}) custom-call(s32[1]{0:T(128)S(6)} %copy.15.length_hbm, bf16[256,3584]{1,0:T(8,128)(2,1)} %tokens_hbm.1, f32[3584]{0:T(1024)} %gain_hbm.1, bf16[3584,896]{1,0:T(8,128)(2,1)} %wq_hbm.1, f32[896]{0:T(1024)} %qb_hbm.1, bf16[3584,128]{1,0:T(8,128)(2,1)} %wk_hbm.1, f32[128]{0:T(128)} %kb_hbm.1, ...), custom_call_target="tpu_custom_call" | custom-call | tf_op jit(solution)/shard_map/pallas_call | solution.py:635
  45.0 0.8 %shard_map.141 = (bf16[256,896]{1,0:T(8,128)(2,1)}, f32[896]{0:T(1024)}) custom-call(bf16[256,896]{1,0:T(8,128)(2,1)S(1)} %get-tuple-element.4.hidden_ref, f32[896]{0:T(1024)S(1)} %get-tuple-element.5.emb_ref), custom_call_target="tpu_custom_call" | custom-call | tf_op jit(solution)/shard_map/pallas_call | solution.py:694

commit v6 on v5

--- a/solution.py
+++ b/solution.py
@@ -261,8 +261,7 @@
         u = rope(u + qb_ref[:, h * HEAD_DIM : (h + 1) * HEAD_DIM]) * HEAD_DIM ** (-0.5)
         qt[:, h * rows : (h + 1) * rows] = jnp.transpose(u.astype(BF16))
 
-    def queries(first):
-        last = min(first + 4, heads)
+    def queries(first, last):
         u = dot(normed[...], wq[:, first * HEAD_DIM : last * HEAD_DIM])
         for h in range(first, last):
             put_query(h, u[:, (h - first) * HEAD_DIM : (h - first + 1) * HEAD_DIM])
@@ -336,7 +335,7 @@
 
     q_load.wait()
     o_load.start()
-    queries(0)
+    queries(0, heads // 2)
 
     @pl.when(mc == 1)
     def _():
@@ -344,8 +343,7 @@
             for way in (0, 1):
                 send_own(way, turn)
 
-    for first in range(4, heads, 4):
-        queries(first)
+    queries(heads // 2, heads)
     forward(1, 0)
     attend([whole(ms)], group=GROUP)
     forward(1, 1)
@@ -383,7 +381,7 @@
             src_ref=psend.at[d, :, place(i)],
             dst_ref=precv.at[d, :, place(i)],
             send_sem=pair_send.at[0],
-            recv_sem=pair_recv.at[i, d],
+            recv_sem=pair_recv.at[0 if d == 0 else i * (n_y - 1) + d],
             device_id=partner,
             device_id_type=MESH,
         )
@@ -430,9 +428,16 @@
         part_sums(i, 0)
 
     squares = None
+    pltpu.make_async_remote_copy(
+        src_ref=psend.at[0],
+        dst_ref=precv.at[0],
+        send_sem=pair_send.at[0],
+        recv_sem=pair_recv.at[0],
+        device_id=partner,
+        device_id_type=MESH,
+    ).wait_recv()
     for i, (at, wide) in enumerate(chunks):
         mine = pl.ds(pl.multiple_of(mh * share + at, HEAD_DIM), wide)
-        pair_copy(i, 0).wait_recv()
         base = tok[:, mine].astype(F32) + (pown[0, :, place(i)] + precv[0, :, place(i)].astype(F32))
         for d in range(1, n_y):
             cross_copy(i, d).wait_recv()
@@ -679,7 +684,7 @@
             dma((2,)),
             dma((SUBS * (8 * half - 4),)),
             dma((1,)),
-            dma((len(chunks), n_y)),
+            dma((1 + len(chunks) * (n_y - 1),)),
             dma((1,)),
             dma((len(chunks), n_y - 1)),
             dma((2,)),

time: 46.1 us -> 46 us (level)
  no operation moved by 1% of the time
where the time goes in v6:
time: 46 us; the launch traced here: 45.9 us
  Pallas kernels  44.4 us (97%)
  between operations  1.45 us (3%)
    pallas_call x1, Pallas kernels, body(): pl.pallas_call(functools.partial(kernel, n_seq, n_head), out_shape=shapes...  43.7 us

profile of v6, /device:TPU:0, one launch (start us, length us, event | category | flops | bytes accessed | tf_op | source)
XLA Modules:
  0.0 45.9 jit_solution(17340422298174319017)
XLA Ops:
  1.3 43.7 %shard_map.140 = (bf16[256,896]{1,0:T(8,128)(2,1)S(1)}, f32[896]{0:T(1024)S(1)}) custom-call(s32[1]{0:T(128)S(6)} %copy.15.length_hbm, bf16[256,3584]{1,0:T(8,128)(2,1)} %tokens_hbm.1, f32[3584]{0:T(1024)} %gain_hbm.1, bf16[3584,896]{1,0:T(8,128)(2,1)} %wq_hbm.1, f32[896]{0:T(1024)} %qb_hbm.1, bf16[3584,128]{1,0:T(8,128)(2,1)} %wk_hbm.1, f32[128]{0:T(128)} %kb_hbm.1, ...), custom_call_target="tpu_custom_call" | custom-call | tf_op jit(solution)/shard_map/pallas_call | solution.py:640
  44.9 0.8 %shard_map.141 = (bf16[256,896]{1,0:T(8,128)(2,1)}, f32[896]{0:T(1024)}) custom-call(bf16[256,896]{1,0:T(8,128)(2,1)S(1)} %get-tuple-element.4.hidden_ref, f32[896]{0:T(1024)S(1)} %get-tuple-element.5.emb_ref), custom_call_target="tpu_custom_call" | custom-call | tf_op jit(solution)/shard_map/pallas_call | solution.py:699
